TPU v7x, 32 devices: a whole 2x2x4 slice. The times are simulated.
32 devices in a mesh: gx: 4 (over y, core), gy: 2 (over x), gz: 4 (over z).
Axes of the slice: x: 2, y: 2, z: 4, core: 2. Of those that a mesh axis runs over, the one named last changes fastest.
Arguments:
- populations: float32 [19, 32, 32, 512], P(None, 'gx', 'gy', 'gz'), may hold values from 0 to 1, as said below
- solid_fraction: float32 [32, 32, 512], P('gx', 'gy', 'gz'), may hold values from 0 to 1
- intersection: int32 [32, 32, 512], P('gx', 'gy', 'gz'), may hold values from 0 to 256, as said below
- touch: int32 [4, 2, 4, 256], P('gx', 'gy', 'gz'), may hold values from 0 to 3455, as said below
- particles: float32 [4, 2, 4, 6, 128], P('gx', 'gy', 'gz'), may hold values from -8 to 8, as said below
- contacts: int32 [4, 2, 4, 12, 128], P('gx', 'gy', 'gz'), may hold values from 0 to 3456, as said below
- dest_code: int32 [4, 2, 4, 128], P('gx', 'gy', 'gz'), may hold values from 4 to 22, as said below
- dest_slot: int32 [4, 2, 4, 128], P('gx', 'gy', 'gz'), may hold values from 0 to 127, as said below
Outputs:
- populations_next: float32 [19, 32, 32, 512], P(None, 'gx', 'gy', 'gz')
- particles_next: float32 [4, 2, 4, 6, 128], P('gx', 'gy', 'gz')
Inputs may be any that keep to these rules, and one draw needn't show every extreme that they name: intersection = 256 marks a cell that no sphere covers; otherwise a touch slot of the cell's block. `touch`: entry o * 128 + s names slot s of the block at offset o of the 27 neighbouring blocks, offsets ordered with x slowest; the entries of one block are distinct and name every slot of the block itself. `contacts`: 3456 marks an empty entry. `dest_code`: a sphere stays (code 13) or moves one block along one axis (codes 4, 10, 12, 14, 16, 22), never out of the mesh; every slot of every block receives exactly one record. `dest_slot`: see dest_code. `populations`: every population is positive. `particles`: positions, in radii from the block centre, lie within the block's half widths; speeds lie within -1.5 to 1.5.
All inputs are finite; a program needn't handle non-finite values.
Results may differ from a plain program's by a relative error of at most 0.000076.
Values sent between devices are 32-bit elements; how exact they have to be, the bound alone decides.
A program may use at most 128 MiB of HBM per device.

v0:
```python
import functools

import jax
import jax.numpy as jnp
from jax import lax
from jax.experimental import pallas as pl
from jax.experimental.pallas import tpu as pltpu
from jax.sharding import PartitionSpec as P

R = 8

LATTICE = [
    (0, 0, 0),
    (1, 0, 0),
    (-1, 0, 0),
    (0, 1, 0),
    (0, -1, 0),
    (0, 0, 1),
    (0, 0, -1),
    (1, 1, 0),
    (-1, -1, 0),
    (1, -1, 0),
    (-1, 1, 0),
    (1, 0, 1),
    (-1, 0, -1),
    (1, 0, -1),
    (-1, 0, 1),
    (0, 1, 1),
    (0, -1, -1),
    (0, 1, -1),
    (0, -1, 1),
]
OPPOSITE = [0, 2, 1, 4, 3, 6, 5, 8, 7, 10, 9, 12, 11, 14, 13, 16, 15, 18, 17]
WEIGHTS = [1.0 / 3.0] + [1.0 / 18.0] * 6 + [1.0 / 36.0] * 12
RELAX_TIME = 0.8
SPEED_UNIT = 0.05
FORCE_SCALE = 0.1
CONTACT_GAIN = 1.0
GRAVITY_STEP = 0.1

MESH = pl.DeviceIdType.MESH
F32 = jnp.float32
BF16 = jnp.bfloat16
I32 = jnp.int32

LEAVING = {
    (axis, sign): [i for i, c in enumerate(LATTICE) if c[axis] == sign]
    for axis in range(3)
    for sign in (1, -1)
}
ORDER = LEAVING[0, 1] + LEAVING[0, -1] + [i for i, c in enumerate(LATTICE) if c[0] == 0]
PLACE = {i: n for n, i in enumerate(ORDER)}
HALOS = [c for c in LATTICE if c != (0, 0, 0)]
HALO_ID = {c: n for n, c in enumerate(HALOS)}
PASS_ORDER = sorted(range(19), key=lambda i: (LATTICE[i][2] != 0, i))
TILES = [c for c in HALOS if c[2] != 0] + [c for c in HALOS if c[2] == 0 and c[0] != 0 and c[1] != 0]
TILE_ID = {c: n for n, c in enumerate(TILES)}
FACES = [(1, 0, 0), (-1, 0, 0), (0, 1, 0), (0, -1, 0), (0, 0, 1), (0, 0, -1)]
LO = 8
GRANT = 16 * 2**20
SUM_UNROLL = 4
COLLIDE_UNROLL = 2


def side(sign):
    return 0 if sign == 1 else 1


def lane_take(table, index):
    return jnp.take_along_axis(table, index, axis=1, mode="promise_in_bounds")


def nt_dot(left, right):
    return lax.dot_general(left, right, (((1,), (1,)), ((), ())), preferred_element_type=F32)


def split_pair(value):
    high = value.astype(BF16).astype(F32)
    return high, value - high


def kernel(
    sizes,
    shape,
    pops_hbm, frac_hbm, inter_hbm, touch_hbm, part_hbm, cont_hbm, code_hbm, slot_hbm,
    rel, xhalo, yhalo, thalo, moved,
    pv, fv, iv, tv, cv, codev, slotv,
    recs, state, sums, fsend, frecv, ypack, zpack, msend, mrecv,
    in_sem, a_send, a_recv, f_send, f_recv, h_send, h_recv, m_send, m_recv,
):
    X, Y, Z = shape
    slots = recs.shape[3]
    touches = tv.shape[1]
    neighbours = cv.shape[0]
    chunks = X * Y // 8
    halves = Y // 8
    me = tuple(lax.axis_index(a) for a in ("gx", "gy", "gz"))

    ins = [
        pltpu.make_async_copy(src, dst, in_sem.at[n])
        for n, (src, dst) in enumerate(
            [
                (part_hbm, recs.at[13]), (pops_hbm, pv), (frac_hbm, fv), (inter_hbm, iv),
                (touch_hbm, tv), (cont_hbm, cv), (code_hbm, codev), (slot_hbm, slotv),
            ]
        )
    ]

    there = {
        (axis, sign): (me[axis] < sizes[axis] - 1) if sign == 1 else (me[axis] > 0)
        for axis in range(3)
        for sign in (1, -1)
    }

    def exists(vector):
        flags = [there[axis, step] for axis, step in enumerate(vector) if step]
        return functools.reduce(lambda p, q: p & q, flags)

    def device(vector):
        return tuple(position + step for position, step in zip(me, vector))

    def each_neighbour(action):
        for o in range(27):
            if o != 13:
                vector = (o // 9 - 1, (o // 3) % 3 - 1, o % 3 - 1)
                pl.when(exists(vector))(functools.partial(action, o, vector))

    for o in range(27):
        if o != 13:
            recs[o] = jnp.zeros(recs.shape[1:], F32)
        frecv[o] = jnp.zeros(frecv.shape[1:], F32)
    for m in range(len(FACES)):
        mrecv[m] = jnp.zeros(mrecv.shape[1:], F32)
    for copy in ins:
        copy.start()

    barrier = pltpu.get_barrier_semaphore()

    def greet(o, vector):
        pl.semaphore_signal(barrier, inc=1, device_id=device(vector), device_id_type=MESH)

    each_neighbour(greet)

    def reach(position, size):
        return 1 + (position > 0).astype(I32) + (position < size - 1).astype(I32)

    count = reach(me[0], sizes[0]) * reach(me[1], sizes[1]) * reach(me[2], sizes[2]) - 1

    ins[0].wait()
    pl.semaphore_wait(barrier, count)

    def record_copy(o, vector):
        return pltpu.make_async_remote_copy(
            src_ref=recs.at[13], dst_ref=recs.at[26 - o], send_sem=a_send.at[o],
            recv_sem=a_recv.at[26 - o], device_id=device(vector), device_id_type=MESH,
        )

    each_neighbour(lambda o, v: record_copy(o, v).start())

    for copy in ins[1:]:
        copy.wait()

    sub8 = lax.broadcasted_iota(I32, (8, Z), 0)
    lane8 = lax.broadcasted_iota(I32, (8, Z), 1)
    high_count = touches // LO
    sub_high = lax.broadcasted_iota(I32, (high_count, Z), 0)

    def gather_pieces(r):
        rows = pl.ds(pl.multiple_of(r * 8, 8), 8)
        f = [pv[i, rows, :] for i in range(19)]
        rho = functools.reduce(lambda a, b: a + b, f)
        momentum = []
        for axis in range(3):
            terms = None
            for i in LEAVING[axis, 1]:
                diff = f[i] - f[OPPOSITE[i]]
                terms = diff if terms is None else terms + diff
            momentum.append(terms)
        index = iv[rows, :]
        eps = fv[rows, :]
        weight = jnp.where(
            index < touches,
            eps * (RELAX_TIME - 0.5) / (1.0 - eps + (RELAX_TIME - 0.5)),
            F32(0.0),
        )
        inverse = 1.0 / rho
        state[0, rows, :] = rho
        for axis in range(3):
            state[1 + axis, rows, :] = momentum[axis] * inverse
        state[4, rows, :] = weight
        wanted = [weight * m for m in momentum] + [weight * rho]
        pairs = [split_pair(w) for w in wanted]
        pieces = [p[0] for p in pairs] + [p[1] for p in pairs]
        high = index // LO if LO & (LO - 1) else lax.shift_right_logical(index, LO.bit_length() - 1)
        low = index - high * LO
        left, right = [], []
        for row in range(8):
            high_row = jnp.broadcast_to(high[row : row + 1], (high_count, Z))
            low_row = jnp.broadcast_to(low[row : row + 1], (8, Z))
            left.append(jnp.where(high_row == sub_high, F32(1.0), F32(0.0)).astype(BF16))
            match = low_row == sub8
            right.append(
                jnp.concatenate(
                    [
                        jnp.where(match, jnp.broadcast_to(p[row : row + 1], (8, Z)), F32(0.0))
                        for p in pieces
                    ],
                    axis=0,
                ).astype(BF16)
            )
        return right, left

    def gather_sums(step, total):
        right, left = [], []
        for n in range(SUM_UNROLL):
            more_right, more_left = gather_pieces(step * SUM_UNROLL + n)
            right += more_right
            left += more_left
        return total + nt_dot(jnp.concatenate(right, axis=1), jnp.concatenate(left, axis=1))

    total = lax.fori_loop(
        0, chunks // SUM_UNROLL, gather_sums, jnp.zeros((8 * LO, high_count), F32)
    )
    sums[...] = jnp.zeros(sums.shape, F32)
    sums[:, 0:high_count] = total[0 : 4 * LO] + total[4 * LO : 8 * LO]

    groups = touches // Z
    parts = []
    for g in range(groups):
        k = lane8 + g * Z
        k_high = lax.shift_right_logical(k, LO.bit_length() - 1)
        k_low = k - k_high * LO
        lines = []
        for q in range(4):
            taken = lane_take(sums[q * LO : (q + 1) * LO, :], k_high)
            lines.append(jnp.sum(jnp.where(k_low == sub8, taken, F32(0.0)), axis=0, keepdims=True))
        quad = jnp.concatenate(lines, axis=0)
        first, second = split_pair(quad)
        parts.append(jnp.concatenate([first, second], axis=0))
    table = jnp.concatenate(parts, axis=1)
    touch_row = tv[...]
    touch_block = lax.shift_right_logical(touch_row, slots.bit_length() - 1)
    touch_slot = touch_row - touch_block * slots
    block8 = jnp.broadcast_to(touch_block, (8, touches))
    spread_left = jnp.concatenate(
        [jnp.where(block8 == o, table, F32(0.0)) for o in range(27)], axis=0
    ).astype(BF16)
    pick = jnp.where(
        jnp.broadcast_to(touch_slot, (slots, touches))
        == lax.broadcasted_iota(I32, (slots, touches), 0),
        F32(1.0),
        F32(0.0),
    ).astype(BF16)
    spread = nt_dot(spread_left, pick)
    for o in range(27):
        piece = spread[o * 8 : (o + 1) * 8]
        fsend[o] = piece + pltpu.roll(piece, 4, 0)

    def force_copy(o, vector):
        return pltpu.make_async_remote_copy(
            src_ref=fsend.at[o], dst_ref=frecv.at[26 - o], send_sem=f_send.at[o],
            recv_sem=f_recv.at[26 - o], device_id=device(vector), device_id_type=MESH,
        )

    each_neighbour(lambda o, v: force_copy(o, v).start())

    code = codev[...]
    wanted_codes = [9 * (v[0] + 1) + 3 * (v[1] + 1) + v[2] + 1 for v in FACES] + [13]
    slot_id = lax.broadcasted_iota(I32, (8, slots), 1).astype(F32) + 1.0
    code_of = jnp.full((8, slots), 27, I32)
    row_id = lax.broadcasted_iota(I32, (8, slots), 0)
    for n, c in enumerate(wanted_codes):
        code_of = jnp.where(row_id == n, c, code_of)
    route = jnp.where(jnp.broadcast_to(code, (8, slots)) == code_of, slot_id, F32(0.0)).astype(BF16)
    place = jnp.where(
        jnp.broadcast_to(slotv[...], (slots, slots)) == lax.broadcasted_iota(I32, (slots, slots), 0),
        F32(1.0),
        F32(0.0),
    ).astype(BF16)
    taken_from = nt_dot(route, place).astype(I32)

    each_neighbour(lambda o, v: record_copy(26 - o, tuple(-s for s in v)).wait_recv())

    index_rows = [touch_row[:, g * Z : (g + 1) * Z] for g in range(groups)]
    touch8 = jnp.concatenate(
        index_rows + [jnp.full((8 - groups, Z), 27 * slots, I32)], axis=0
    )

    def fetch(first_row, index):
        found = [jnp.zeros((8, Z), F32)] * 3
        block = lax.shift_right_logical(index, slots.bit_length() - 1)
        local = index - block * slots
        for o in range(27):
            hit = block == o
            for d in range(3):
                row = jnp.broadcast_to(recs[o, first_row + d], (8, Z))
                found[d] = jnp.where(hit, lane_take(row, local), found[d])
        return found

    touch_velocity = [SPEED_UNIT * v for v in fetch(3, touch8)]
    tables = [
        [jnp.broadcast_to(touch_velocity[d][g : g + 1], (8, Z)) for g in range(groups)]
        for d in range(3)
    ]

    def collide(r):
        rows = pl.ds(pl.multiple_of(r * 8, 8), 8)
        rho = state[0, rows, :]
        u = [state[1 + d, rows, :] for d in range(3)]
        weight = state[4, rows, :]
        index = iv[rows, :]
        group = lax.shift_right_logical(index, Z.bit_length() - 1)
        local = index - group * Z
        v = []
        for d in range(3):
            value = jnp.zeros((8, Z), F32)
            for g in range(groups):
                value = jnp.where(group == g, lane_take(tables[d][g], local), value)
            v.append(value)
        keep = (1.0 - weight) * (1.0 / RELAX_TIME)
        rest_u = 1.0 - 1.5 * (u[0] * u[0] + u[1] * u[1] + u[2] * u[2])
        rest_v = 1.0 - 1.5 * (v[0] * v[0] + v[1] * v[1] + v[2] * v[2])
        scaled = {w: w * rho for w in sorted(set(WEIGHTS))}
        f0 = pv[0, rows, :]
        eq_u = scaled[WEIGHTS[0]] * rest_u
        eq_v = scaled[WEIGHTS[0]] * rest_v
        rel[PLACE[0], rows, :] = f0 - keep * (f0 - eq_u) + weight * (eq_v - eq_u)

        def dot(c, vec):
            value = None
            for axis in range(3):
                if c[axis]:
                    term = vec[axis] if c[axis] == 1 else -vec[axis]
                    value = term if value is None else value + term
            return value

        for i in range(1, 19, 2):
            j = OPPOSITE[i]
            share = scaled[WEIGHTS[i]]
            pu, ps = dot(LATTICE[i], u), dot(LATTICE[i], v)
            even_u = share * (rest_u + 4.5 * pu * pu)
            odd_u = share * (3.0 * pu)
            even_v = share * (rest_v + 4.5 * ps * ps)
            odd_v = share * (3.0 * ps)
            fi, fj = pv[i, rows, :], pv[j, rows, :]
            ui, uj = even_u + odd_u, even_u - odd_u
            diff = fj - fi
            rel[PLACE[i], rows, :] = fi - keep * (fi - ui) + weight * (diff + (even_v + odd_v) - uj)
            rel[PLACE[j], rows, :] = fj - keep * (fj - uj) + weight * ((even_v - odd_v) - ui - diff)

    def collide_some(step, carry):
        for n in range(COLLIDE_UNROLL):
            collide(step * COLLIDE_UNROLL + n)
        return carry

    lax.fori_loop(0, chunks // COLLIDE_UNROLL, collide_some, 0)

    def halo_copy(vector):
        m = HALO_ID[vector]
        if vector[2] != 0:
            src, dst = zpack.at[side(vector[2])], thalo.at[TILE_ID[vector]]
        elif vector[0] != 0 and vector[1] != 0:
            entry = LEAVING[1, vector[1]].index(LATTICE.index(vector))
            src, dst = ypack.at[side(vector[1]), entry], thalo.at[TILE_ID[vector]]
        elif vector[0] != 0:
            start = 5 * side(vector[0])
            row = (X - 1) * Y if vector[0] == 1 else 0
            src = rel.at[pl.ds(start, 5), pl.ds(row, Y), :]
            dst = xhalo.at[side(vector[0])]
        else:
            src, dst = ypack.at[side(vector[1])], yhalo.at[side(vector[1])]
        return pltpu.make_async_remote_copy(
            src_ref=src, dst_ref=dst, send_sem=h_send.at[m], recv_sem=h_recv.at[m],
            device_id=device(vector), device_id_type=MESH,
        )

    def when_there(vector, action):
        pl.when(exists(vector))(action)

    for vector in HALOS:
        if vector[1] == 0 and vector[2] == 0:
            when_there(vector, lambda vector=vector: halo_copy(vector).start())
    for sign in (1, -1):
        for entry, i in enumerate(LEAVING[1, sign]):
            first = Y - 1 if sign == 1 else 0
            ypack[side(sign), entry] = rel[PLACE[i], pl.ds(first, X, stride=Y), :]
    for vector in HALOS:
        if vector[1] != 0 and vector[2] == 0:
            when_there(vector, lambda vector=vector: halo_copy(vector).start())
    for sign in (1, -1):
        edge = Z - 1 if sign == 1 else 0
        packed = jnp.zeros((8, Z), F32)
        for entry, i in enumerate(LEAVING[2, sign]):
            for r in range(chunks):
                column = entry * chunks + r
                turned = rel[PLACE[i], r * 8 : r * 8 + 8, :]
                if (column - edge) % Z:
                    turned = pltpu.roll(turned, (column - edge) % Z, 1)
                packed = jnp.where(lane8 == column, turned, packed)
        zpack[side(sign)] = packed
    for vector in HALOS:
        if vector[2] != 0:
            when_there(vector, lambda vector=vector: halo_copy(vector).start())

    own = [recs[13, d] for d in range(6)]
    contact = [jnp.zeros((1, slots), F32) for _ in range(3)]
    spans = (X / R, Y / R, Z / R)
    for start in range(0, neighbours, 8):
        stop = min(start + 8, neighbours)
        lines = [cv[n] for n in range(start, stop)]
        if stop - start < 8:
            lines.append(jnp.full((8 - stop + start, slots), 27 * slots, I32))
        entries = jnp.concatenate(lines, axis=0)
        found = fetch(0, entries)
        block = lax.shift_right_logical(entries, slots.bit_length() - 1)
        nine = jnp.zeros(block.shape, I32)
        for step in (9, 18, 27):
            nine = nine + (block >= step).astype(I32)
        inner = block - 9 * nine
        three = (inner >= 3).astype(I32) + (inner >= 6).astype(I32)
        moves = (nine - 1, three - 1, inner - 3 * three - 1)
        apart = [
            jnp.broadcast_to(own[d], (8, slots)) - (found[d] + moves[d].astype(F32) * spans[d])
            for d in range(3)
        ]
        soften = 1.0 + 0.25 * (apart[0] * apart[0] + apart[1] * apart[1] + apart[2] * apart[2])
        strength = CONTACT_GAIN * (entries < 27 * slots).astype(F32) / (soften * soften)
        for d in range(3):
            contact[d] = contact[d] + jnp.sum(apart[d] * strength, axis=0, keepdims=True)

    each_neighbour(lambda o, v: force_copy(26 - o, tuple(-s for s in v)).wait_recv())
    force = fsend[13]
    for o in range(27):
        if o != 13:
            force = force + frecv[o]
    gravity = (0.0, 0.0, GRAVITY_STEP)
    velocity_new, position_new = [], []
    for d in range(3):
        speed = own[3 + d]
        hydro = force[d : d + 1] - force[3:4] * (SPEED_UNIT * speed)
        velocity = speed + FORCE_SCALE * hydro + contact[d] - gravity[d]
        velocity_new.append(velocity)
        position_new.append(own[d] + velocity * (SPEED_UNIT / R))
    record = jnp.concatenate(position_new + velocity_new + [jnp.zeros((2, slots), F32)], axis=0)

    def routed(n, vector):
        origin = jnp.broadcast_to(taken_from[n : n + 1], (8, slots))
        moved = lane_take(record, jnp.where(origin > 0, origin - 1, 0))
        shift = jnp.zeros((8, slots), F32)
        for d in range(3):
            if vector[d]:
                shift = jnp.where(row_id == d, F32(vector[d] * spans[d]), shift)
        return jnp.where(origin > 0, moved - shift, F32(0.0))

    def move_copy(n):
        return pltpu.make_async_remote_copy(
            src_ref=msend.at[n], dst_ref=mrecv.at[n], send_sem=m_send.at[n],
            recv_sem=m_recv.at[n], device_id=device(FACES[n]), device_id_type=MESH,
        )

    for n, vector in enumerate(FACES):
        msend[n] = routed(n, vector)
        when_there(vector, lambda n=n: move_copy(n).start())
    stay = routed(6, (0, 0, 0))

    each_neighbour(lambda o, v: record_copy(o, v).wait_send())
    each_neighbour(lambda o, v: force_copy(o, v).wait_send())
    for vector in HALOS:
        when_there(vector, lambda vector=vector: halo_copy(vector).wait_send())
    for vector in HALOS:
        back = tuple(-step for step in vector)
        when_there(back, lambda vector=vector: halo_copy(vector).wait_recv())
    for n, vector in enumerate(FACES):
        back = tuple(-step for step in vector)
        when_there(back, lambda n=n: move_copy(n).wait_recv())
    for n in range(len(FACES)):
        stay = stay + mrecv[n]
    for d in range(6):
        moved[d] = stay[d : d + 1]
    for n, vector in enumerate(FACES):
        when_there(vector, lambda n=n: move_copy(n).wait_send())


def pass_kernel(sizes, shape, rel, xhalo, yhalo, thalo, moved, out_hbm, part_out, pv, out_sem):
    X, Y, Z = shape
    chunks = X * Y // 8
    halves = Y // 8
    me = tuple(lax.axis_index(a) for a in ("gx", "gy", "gz"))
    part_copy = pltpu.make_async_copy(moved, part_out, out_sem.at[len(LATTICE)])
    part_copy.start()
    suby = lax.broadcasted_iota(I32, (Y, Z), 0)
    laney = lax.broadcasted_iota(I32, (Y, Z), 1)
    open_back = {
        (axis, sign): (me[axis] > 0) if sign == 1 else (me[axis] < sizes[axis] - 1)
        for axis in range(3)
        for sign in (1, -1)
    }
    target = {1: 0, -1: Z - 1}
    row_edge = {1: 0, -1: Y - 1}

    def edge_mask(c):
        mask = None
        if c[1]:
            blocked = jnp.broadcast_to(jnp.where(open_back[1, c[1]], -1, row_edge[c[1]]), (Y, Z))
            mask = suby != blocked
        if c[2]:
            blocked = jnp.broadcast_to(jnp.where(open_back[2, c[2]], -1, target[c[2]]), (Y, Z))
            other = laney != blocked
            mask = other if mask is None else mask & other
        return mask

    out_copies = [part_copy]

    for i in PASS_ORDER:
        c = LATTICE[i]
        j = OPPOSITE[i]
        mask = edge_mask(c)
        for x in range(X):
            from_x = x - c[0]
            inside_x = 0 <= from_x < X
            wrapped = from_x % X
            if inside_x:
                slab = rel[PLACE[i], from_x * Y : (from_x + 1) * Y, :]
            else:
                slab = xhalo[side(c[0]), LEAVING[0, c[0]].index(i)]
            turn = 1 if c[2] == 1 else Z - 1
            if c[2]:
                entry = LEAVING[2, c[2]].index(i)
                tile = thalo[TILE_ID[(0, 0, c[2])]] if inside_x else thalo[TILE_ID[(c[0], 0, c[2])]]
                columns = []
                for h in range(halves):
                    column = entry * chunks + wrapped * halves + h
                    amount = (target[c[2]] - column) % Z
                    columns.append(pltpu.roll(tile, amount, 1) if amount else tile)
                edge_columns = jnp.concatenate(columns, axis=0)
                slab = jnp.where(laney == target[c[2]], edge_columns, pltpu.roll(slab, turn, 1))
            if c[1]:
                entry = LEAVING[1, c[1]].index(i)
                if inside_x:
                    line = yhalo[side(c[1]), entry, from_x : from_x + 1, :]
                else:
                    line = thalo[TILE_ID[(c[0], c[1], 0)], wrapped : wrapped + 1, :]
                if c[2]:
                    entry = LEAVING[2, c[2]].index(i)
                    last = (Y - 1) if c[1] == 1 else 0
                    column = entry * chunks + from_x * halves + last // 8
                    amount = (target[c[2]] - column) % Z
                    tile = thalo[TILE_ID[c]]
                    tile = pltpu.roll(tile, amount, 1) if amount else tile
                    corner = tile[last % 8 : last % 8 + 1]
                    tile = yhalo[side(c[1]), LEAVING[1, c[1]].index(i)]
                    line = pltpu.roll(tile, turn, 1)[from_x : from_x + 1]
                    line = jnp.where(laney[0:1] == target[c[2]], corner, line)
                slab = pltpu.roll(slab, 1 if c[1] == 1 else Y - 1, 0)
                slab = jnp.where(suby == row_edge[c[1]], jnp.broadcast_to(line, (Y, Z)), slab)
            mirror = rel[PLACE[j], x * Y : (x + 1) * Y, :] if c != (0, 0, 0) else None
            if mask is not None:
                slab = jnp.where(mask, slab, mirror)
            if not inside_x:
                closed = jnp.broadcast_to(open_back[0, c[0]].astype(I32), (Y, Z))
                slab = jnp.where(closed > 0, slab, mirror)
            pv[i, x * Y : (x + 1) * Y, :] = slab
        copy = pltpu.make_async_copy(pv.at[i], out_hbm.at[i], out_sem.at[i])
        copy.start()
        out_copies.append(copy)

    for copy in out_copies:
        copy.wait()


def body(sizes, populations, solid_fraction, intersection, touch, particles, contacts, dest_code, dest_slot):
    count, X, Y, Z = populations.shape
    slots = particles.shape[4]
    touches = touch.shape[3]
    neighbours = contacts.shape[3]
    any_space = pl.BlockSpec(memory_space=pl.ANY)
    dma = pltpu.SemaphoreType.DMA
    vmem = pl.BlockSpec(memory_space=pltpu.VMEM)
    values = (
        populations.reshape(count, X * Y, Z),
        solid_fraction.reshape(X * Y, Z),
        intersection.reshape(X * Y, Z),
        touch.reshape(1, touches),
        particles.reshape(6, 1, slots),
        contacts.reshape(neighbours, 1, slots),
        dest_code.reshape(1, slots),
        dest_slot.reshape(1, slots),
    )
    handed = pl.pallas_call(
        functools.partial(kernel, sizes, (X, Y, Z)),
        out_shape=(
            pltpu.VMEM((count, X * Y, Z), F32),
            pltpu.VMEM((2, 5, Y, Z), F32),
            pltpu.VMEM((2, 5, X, Z), F32),
            pltpu.VMEM((len(TILES), 8, Z), F32),
            pltpu.VMEM((6, 1, slots), F32),
        ),
        in_specs=[pl.BlockSpec(memory_space=pltpu.HBM)] * 8,
        out_specs=(vmem,) * 5,
        scratch_shapes=[
            pltpu.VMEM((count, X * Y, Z), F32),
            pltpu.VMEM((X * Y, Z), F32),
            pltpu.VMEM((X * Y, Z), I32),
            pltpu.VMEM((1, touches), I32),
            pltpu.VMEM((neighbours, 1, slots), I32),
            pltpu.VMEM((1, slots), I32),
            pltpu.VMEM((1, slots), I32),
            pltpu.VMEM((27, 6, 1, slots), F32),
            pltpu.VMEM((5, X * Y, Z), F32),
            pltpu.VMEM((4 * LO, Z), F32),
            pltpu.VMEM((27, 8, slots), F32),
            pltpu.VMEM((27, 8, slots), F32),
            pltpu.VMEM((2, 5, X, Z), F32),
            pltpu.VMEM((2, 8, Z), F32),
            pltpu.VMEM((len(FACES), 8, slots), F32),
            pltpu.VMEM((len(FACES), 8, slots), F32),
            dma((8,)),
            dma((27,)),
            dma((27,)),
            dma((27,)),
            dma((27,)),
            dma((len(HALOS),)),
            dma((len(HALOS),)),
            dma((len(FACES),)),
            dma((len(FACES),)),
        ],
        compiler_params=pltpu.CompilerParams(
            collective_id=0, has_side_effects=True, vmem_limit_bytes=GRANT
        ),
    )(*[pltpu.with_memory_space_constraint(value, pltpu.HBM) for value in values])
    out, moved = pl.pallas_call(
        functools.partial(pass_kernel, sizes, (X, Y, Z)),
        out_shape=(
            jax.ShapeDtypeStruct((count, X * Y, Z), F32),
            jax.ShapeDtypeStruct((6, 1, slots), F32),
        ),
        in_specs=[vmem] * 5,
        out_specs=(any_space, any_space),
        scratch_shapes=[pltpu.VMEM((count, X * Y, Z), F32), dma((count + 1,))],
        compiler_params=pltpu.CompilerParams(vmem_limit_bytes=GRANT),
    )(*[pltpu.with_memory_space_constraint(value, pltpu.VMEM) for value in handed])
    return (out.reshape(count, X, Y, Z), moved.reshape(1, 1, 1, 6, slots))


def solution(mesh):
    placed = (
        P(None, "gx", "gy", "gz"),
        P("gx", "gy", "gz"),
        P("gx", "gy", "gz"),
        P("gx", "gy", "gz", None),
        P("gx", "gy", "gz", None, None),
        P("gx", "gy", "gz", None, None),
        P("gx", "gy", "gz", None),
        P("gx", "gy", "gz", None),
    )
    sizes = tuple(mesh.shape[axis] for axis in ("gx", "gy", "gz"))
    return jax.shard_map(
        functools.partial(body, sizes),
        mesh=mesh,
        in_specs=placed,
        out_specs=(P(None, "gx", "gy", "gz"), P("gx", "gy", "gz", None, None)),
        check_vma=False,
    )
```

profile of v0, /device:TPU:0, one launch (start us, length us, event | category | flops | bytes accessed | tf_op | source)
XLA Modules:
  0.0 16.8 jit_solution(8418623400966050038)
XLA Ops:
  0.6 14.9 %shard_map.95 = (f32[19,128,128]{2,1,0:T(8,128)S(1)}, f32[2,5,16,128]{3,2,1,0:T(8,128)S(1)}, f32[2,5,8,128]{3,2,1,0:T(8,128)S(1)}, f32[14,8,128]{2,1,0:T(8,128)S(1)}, f32[6,1,128]{2,1,0:T(1,128)S(1)}) custom-call(f32[19,128,128]{2,1,0:T(8,128)} %bitcast.12, f32[128,128]{1,0:T(8,128)} %bitcast.13, s32[128,128]{1,0:T(8,128)} %bitcast.14, s32[1,256]{1,0:T(1,128)} %bitcast.17, ...), custom_call_target="tpu_custom_call" | custom-call | tf_op jit(solution)/shard_map/pallas_call | solution.py:589
  15.5 1.3 %shard_map.96 = (f32[19,128,128]{2,1,0:T(8,128)}, f32[6,1,128]{2,1,0:T(1,128)}) custom-call(f32[19,128,128]{2,1,0:T(8,128)S(1)} %get-tuple-element.9.rel, f32[2,5,16,128]{3,2,1,0:T(8,128)S(1)} %get-tuple-element.10.xhalo, f32[2,5,8,128]{3,2,1,0:T(8,128)S(1)} %get-tuple-element.11.yhalo, f32[14,8,128]{2,1,0:T(8,128)S(1)} %get-tuple-element.12.thalo, ...), custom_call_target="tpu_custom_call" | custom-call | tf_op jit(solution)/shard_map/pallas_call | solution.py:631
where the time goes:
time: 17 us; the launch traced here: 16.8 us
  Pallas kernels  16.2 us (95%)
  between operations  0.64 us (4%)
    pallas_call x1, Pallas kernels, body(): pl.pallas_call(functools.partial(kernel, sizes, (X, Y, Z)), out_shape=(pl...  14.9 us
    pallas_call x1, Pallas kernels, body(): pl.pallas_call(functools.partial(pass_kernel, sizes, (X, Y, Z)), out_shap...  1.29 us

commit v1 on v0

--- a/solution.py
+++ b/solution.py
@@ -1,4 +1,5 @@
 import functools
+import itertools
 
 import jax
 import jax.numpy as jnp
@@ -59,6 +60,7 @@
 LO = 8
 GRANT = 16 * 2**20
 SUM_UNROLL = 4
+EARLY_STEPS = 2
 COLLIDE_UNROLL = 2
 
 
@@ -86,7 +88,7 @@
     rel, xhalo, yhalo, thalo, moved,
     pv, fv, iv, tv, cv, codev, slotv,
     recs, state, sums, fsend, frecv, ypack, zpack, msend, mrecv,
-    in_sem, a_send, a_recv, f_send, f_recv, h_send, h_recv, m_send, m_recv,
+    in_sem, a_sem, f_sem, h_send, h_recv, m_sem,
 ):
     X, Y, Z = shape
     slots = recs.shape[3]
@@ -96,15 +98,23 @@
     halves = Y // 8
     me = tuple(lax.axis_index(a) for a in ("gx", "gy", "gz"))
 
-    ins = [
-        pltpu.make_async_copy(src, dst, in_sem.at[n])
+    own_in = pltpu.make_async_copy(part_hbm, recs.at[13], in_sem.at[0])
+    cell_ins = [
+        pltpu.make_async_copy(inter_hbm, iv, in_sem.at[1]),
+        pltpu.make_async_copy(frac_hbm, fv, in_sem.at[2]),
+    ]
+    small_ins = [
+        pltpu.make_async_copy(src, dst, in_sem.at[3 + n])
         for n, (src, dst) in enumerate(
-            [
-                (part_hbm, recs.at[13]), (pops_hbm, pv), (frac_hbm, fv), (inter_hbm, iv),
-                (touch_hbm, tv), (cont_hbm, cv), (code_hbm, codev), (slot_hbm, slotv),
-            ]
+            [(touch_hbm, tv), (cont_hbm, cv), (code_hbm, codev), (slot_hbm, slotv)]
         )
     ]
+    steps = chunks // SUM_UNROLL
+    span = SUM_UNROLL * 8
+
+    def pops_in(step):
+        rows = pl.ds(pl.multiple_of(step * span, span), span)
+        return pltpu.make_async_copy(pops_hbm.at[:, rows], pv.at[:, rows], in_sem.at[7 + step])
 
     there = {
         (axis, sign): (me[axis] < sizes[axis] - 1) if sign == 1 else (me[axis] > 0)
@@ -125,40 +135,41 @@
                 vector = (o // 9 - 1, (o // 3) % 3 - 1, o % 3 - 1)
                 pl.when(exists(vector))(functools.partial(action, o, vector))
 
-    for o in range(27):
-        if o != 13:
-            recs[o] = jnp.zeros(recs.shape[1:], F32)
-        frecv[o] = jnp.zeros(frecv.shape[1:], F32)
-    for m in range(len(FACES)):
-        mrecv[m] = jnp.zeros(mrecv.shape[1:], F32)
-    for copy in ins:
-        copy.start()
-
+    own_in.start()
     barrier = pltpu.get_barrier_semaphore()
 
     def greet(o, vector):
         pl.semaphore_signal(barrier, inc=1, device_id=device(vector), device_id_type=MESH)
 
     each_neighbour(greet)
-
-    def reach(position, size):
-        return 1 + (position > 0).astype(I32) + (position < size - 1).astype(I32)
-
-    count = reach(me[0], sizes[0]) * reach(me[1], sizes[1]) * reach(me[2], sizes[2]) - 1
-
-    ins[0].wait()
-    pl.semaphore_wait(barrier, count)
+    for copy in cell_ins:
+        copy.start()
+    for step in range(steps):
+        pops_in(step).start()
+    for copy in small_ins:
+        copy.start()
+
+    around = [
+        (me[axis] > 0).astype(I32) + (me[axis] < sizes[axis] - 1).astype(I32) for axis in range(3)
+    ]
+    options = [[0] if size == 1 else [1] if size == 2 else [1, 2] for size in sizes]
+    nearby = lambda n: (n[0] + 1) * (n[1] + 1) * (n[2] + 1) - 1
+    tiles_near = lambda n: n[2] + n[0] * n[1] + n[0] * n[2] + n[1] * n[2]
+    faces_near = lambda n: n[0] + n[1] + n[2]
+    count = nearby(around)
+
+    def wait_all(measure, ref, semaphore):
+        amount = measure(around)
+        for c in sorted({measure(n) for n in itertools.product(*options)}):
+            if c:
+                part = ref.at[pl.ds(0, c)]
+                pl.when(amount == c)(lambda part=part: pltpu.make_async_copy(part, part, semaphore).wait())
 
     def record_copy(o, vector):
         return pltpu.make_async_remote_copy(
-            src_ref=recs.at[13], dst_ref=recs.at[26 - o], send_sem=a_send.at[o],
-            recv_sem=a_recv.at[26 - o], device_id=device(vector), device_id_type=MESH,
-        )
-
-    each_neighbour(lambda o, v: record_copy(o, v).start())
-
-    for copy in ins[1:]:
-        copy.wait()
+            src_ref=recs.at[13], dst_ref=recs.at[26 - o], send_sem=a_sem.at[0],
+            recv_sem=a_sem.at[1], device_id=device(vector), device_id_type=MESH,
+        )
 
     sub8 = lax.broadcasted_iota(I32, (8, Z), 0)
     lane8 = lax.broadcasted_iota(I32, (8, Z), 1)
@@ -189,6 +200,7 @@
             state[1 + axis, rows, :] = momentum[axis] * inverse
         state[4, rows, :] = weight
         wanted = [weight * m for m in momentum] + [weight * rho]
+        state[5, rows, :] = wanted[3]
         pairs = [split_pair(w) for w in wanted]
         pieces = [p[0] for p in pairs] + [p[1] for p in pairs]
         high = index // LO if LO & (LO - 1) else lax.shift_right_logical(index, LO.bit_length() - 1)
@@ -211,6 +223,7 @@
         return right, left
 
     def gather_sums(step, total):
+        pops_in(step).wait()
         right, left = [], []
         for n in range(SUM_UNROLL):
             more_right, more_left = gather_pieces(step * SUM_UNROLL + n)
@@ -218,9 +231,19 @@
             left += more_left
         return total + nt_dot(jnp.concatenate(right, axis=1), jnp.concatenate(left, axis=1))
 
-    total = lax.fori_loop(
-        0, chunks // SUM_UNROLL, gather_sums, jnp.zeros((8 * LO, high_count), F32)
-    )
+    for copy in cell_ins:
+        copy.wait()
+    total = jnp.zeros((8 * LO, high_count), F32)
+    if EARLY_STEPS:
+        total = lax.fori_loop(0, EARLY_STEPS, gather_sums, total)
+
+    own_in.wait()
+    pl.semaphore_wait(barrier, count)
+    each_neighbour(lambda o, v: record_copy(o, v).start())
+
+    total = lax.fori_loop(EARLY_STEPS, steps, gather_sums, total)
+    for copy in small_ins:
+        copy.wait()
     sums[...] = jnp.zeros(sums.shape, F32)
     sums[:, 0:high_count] = total[0 : 4 * LO] + total[4 * LO : 8 * LO]
 
@@ -254,15 +277,31 @@
     spread = nt_dot(spread_left, pick)
     for o in range(27):
         piece = spread[o * 8 : (o + 1) * 8]
-        fsend[o] = piece + pltpu.roll(piece, 4, 0)
+        fsend[o] = (piece + pltpu.roll(piece, 4, 0))[0:4]
 
     def force_copy(o, vector):
         return pltpu.make_async_remote_copy(
-            src_ref=fsend.at[o], dst_ref=frecv.at[26 - o], send_sem=f_send.at[o],
-            recv_sem=f_recv.at[26 - o], device_id=device(vector), device_id_type=MESH,
+            src_ref=fsend.at[o], dst_ref=frecv.at[26 - o], send_sem=f_sem.at[0],
+            recv_sem=f_sem.at[1], device_id=device(vector), device_id_type=MESH,
         )
 
     each_neighbour(lambda o, v: force_copy(o, v).start())
+
+    def clear(o):
+        recs[o] = jnp.zeros(recs.shape[1:], F32)
+        frecv[o] = jnp.zeros(frecv.shape[1:], F32)
+
+    for o in range(27):
+        if o != 13:
+            vector = (o // 9 - 1, (o // 3) % 3 - 1, o % 3 - 1)
+            pl.when(jnp.logical_not(exists(vector)))(functools.partial(clear, o))
+    for n, vector in enumerate(FACES):
+        back = tuple(-step for step in vector)
+
+        def clear_moved(n=n):
+            mrecv[n] = jnp.zeros(mrecv.shape[1:], F32)
+
+        pl.when(jnp.logical_not(exists(back)))(clear_moved)
 
     code = codev[...]
     wanted_codes = [9 * (v[0] + 1) + 3 * (v[1] + 1) + v[2] + 1 for v in FACES] + [13]
@@ -279,7 +318,78 @@
     ).astype(BF16)
     taken_from = nt_dot(route, place).astype(I32)
 
-    each_neighbour(lambda o, v: record_copy(26 - o, tuple(-s for s in v)).wait_recv())
+    def dot(c, vec):
+        value = None
+        for axis in range(3):
+            if c[axis]:
+                term = vec[axis] if c[axis] == 1 else -vec[axis]
+                value = term if value is None else value + term
+        return value
+
+    def collide_fluid(r):
+        rows = pl.ds(pl.multiple_of(r * 8, 8), 8)
+        rho = state[0, rows, :]
+        u = [state[1 + d, rows, :] for d in range(3)]
+        weight = state[4, rows, :]
+        keep = (1.0 - weight) * (1.0 / RELAX_TIME)
+        rest_u = 1.0 - 1.5 * (u[0] * u[0] + u[1] * u[1] + u[2] * u[2])
+        scaled = {w: w * rho for w in sorted(set(WEIGHTS))}
+        f0 = pv[0, rows, :]
+        eq_u = scaled[WEIGHTS[0]] * rest_u
+        rel[PLACE[0], rows, :] = f0 - keep * (f0 - eq_u) - weight * eq_u
+        for i in range(1, 19, 2):
+            j = OPPOSITE[i]
+            share = scaled[WEIGHTS[i]]
+            pu = dot(LATTICE[i], u)
+            even = share * (rest_u + 4.5 * pu * pu)
+            odd = share * (3.0 * pu)
+            fi, fj = pv[i, rows, :], pv[j, rows, :]
+            ui, uj = even + odd, even - odd
+            diff = fj - fi
+            rel[PLACE[i], rows, :] = fi - keep * (fi - ui) + weight * (diff - uj)
+            rel[PLACE[j], rows, :] = fj - keep * (fj - uj) - weight * (diff + ui)
+
+    def collide_some(step, carry):
+        for n in range(COLLIDE_UNROLL):
+            collide_fluid(step * COLLIDE_UNROLL + n)
+        return carry
+
+    lax.fori_loop(0, chunks // COLLIDE_UNROLL, collide_some, 0)
+
+    edges = {(axis, sign): n for n, (axis, sign) in enumerate([(1, 1), (1, -1), (2, 1), (2, -1)])}
+    edge_index, edge_share, line_of = {}, {}, {}
+    for sign in (1, -1):
+        line = pl.ds(Y - 1 if sign == 1 else 0, X, stride=Y)
+        for entry, i in enumerate(LEAVING[1, sign]):
+            ypack[side(sign), entry] = rel[PLACE[i], line, :]
+        line_of[sign] = line
+
+    def pack_columns(read, entries, edge, start):
+        packed = start
+        for entry in range(entries):
+            for r in range(chunks):
+                column = entry * chunks + r
+                turned = read(entry, pl.ds(r * 8, 8))
+                if (column - edge) % Z:
+                    turned = pltpu.roll(turned, (column - edge) % Z, 1)
+                packed = jnp.where(lane8 == column, turned, packed)
+        return packed
+
+    repeat = lax.rem(lane8, chunks)
+    for sign in (1, -1):
+        edge = Z - 1 if sign == 1 else 0
+        leaving = LEAVING[2, sign]
+        zpack[side(sign)] = pack_columns(
+            lambda entry, rows: rel[PLACE[leaving[entry]], rows, :], 5, edge, jnp.zeros((8, Z), F32)
+        )
+        share = pack_columns(lambda entry, rows: state[5, rows, :], 1, edge, jnp.zeros((8, Z), F32))
+        index = pack_columns(
+            lambda entry, rows: iv[rows, :], 1, edge, jnp.full((8, Z), touches, I32)
+        )
+        edge_share[sign] = lane_take(share, repeat)
+        edge_index[sign] = lane_take(index, repeat)
+
+    wait_all(nearby, recs, a_sem.at[1])
 
     index_rows = [touch_row[:, g * Z : (g + 1) * Z] for g in range(groups)]
     touch8 = jnp.concatenate(
@@ -303,12 +413,7 @@
         for d in range(3)
     ]
 
-    def collide(r):
-        rows = pl.ds(pl.multiple_of(r * 8, 8), 8)
-        rho = state[0, rows, :]
-        u = [state[1 + d, rows, :] for d in range(3)]
-        weight = state[4, rows, :]
-        index = iv[rows, :]
+    def solid_velocity(index):
         group = lax.shift_right_logical(index, Z.bit_length() - 1)
         local = index - group * Z
         v = []
@@ -317,46 +422,10 @@
             for g in range(groups):
                 value = jnp.where(group == g, lane_take(tables[d][g], local), value)
             v.append(value)
-        keep = (1.0 - weight) * (1.0 / RELAX_TIME)
-        rest_u = 1.0 - 1.5 * (u[0] * u[0] + u[1] * u[1] + u[2] * u[2])
-        rest_v = 1.0 - 1.5 * (v[0] * v[0] + v[1] * v[1] + v[2] * v[2])
-        scaled = {w: w * rho for w in sorted(set(WEIGHTS))}
-        f0 = pv[0, rows, :]
-        eq_u = scaled[WEIGHTS[0]] * rest_u
-        eq_v = scaled[WEIGHTS[0]] * rest_v
-        rel[PLACE[0], rows, :] = f0 - keep * (f0 - eq_u) + weight * (eq_v - eq_u)
-
-        def dot(c, vec):
-            value = None
-            for axis in range(3):
-                if c[axis]:
-                    term = vec[axis] if c[axis] == 1 else -vec[axis]
-                    value = term if value is None else value + term
-            return value
-
-        for i in range(1, 19, 2):
-            j = OPPOSITE[i]
-            share = scaled[WEIGHTS[i]]
-            pu, ps = dot(LATTICE[i], u), dot(LATTICE[i], v)
-            even_u = share * (rest_u + 4.5 * pu * pu)
-            odd_u = share * (3.0 * pu)
-            even_v = share * (rest_v + 4.5 * ps * ps)
-            odd_v = share * (3.0 * ps)
-            fi, fj = pv[i, rows, :], pv[j, rows, :]
-            ui, uj = even_u + odd_u, even_u - odd_u
-            diff = fj - fi
-            rel[PLACE[i], rows, :] = fi - keep * (fi - ui) + weight * (diff + (even_v + odd_v) - uj)
-            rel[PLACE[j], rows, :] = fj - keep * (fj - uj) + weight * ((even_v - odd_v) - ui - diff)
-
-    def collide_some(step, carry):
-        for n in range(COLLIDE_UNROLL):
-            collide(step * COLLIDE_UNROLL + n)
-        return carry
-
-    lax.fori_loop(0, chunks // COLLIDE_UNROLL, collide_some, 0)
+        return v, 1.0 - 1.5 * (v[0] * v[0] + v[1] * v[1] + v[2] * v[2])
 
     def halo_copy(vector):
-        m = HALO_ID[vector]
+        m = 2 if vector[2] != 0 or (vector[0] != 0 and vector[1] != 0) else 0 if vector[0] != 0 else 1
         if vector[2] != 0:
             src, dst = zpack.at[side(vector[2])], thalo.at[TILE_ID[vector]]
         elif vector[0] != 0 and vector[1] != 0:
@@ -377,29 +446,52 @@
     def when_there(vector, action):
         pl.when(exists(vector))(action)
 
+    entry8 = lane8 // chunks
+    for sign in (1, -1):
+        v, rest = solid_velocity(edge_index[sign])
+        along = v[2] if sign == 1 else -v[2]
+        base = jnp.zeros((8, Z), F32)
+        for entry, i in enumerate(LEAVING[2, sign]):
+            here = entry8 == entry
+            base = jnp.where(here, F32(WEIGHTS[i]), base)
+            for d in range(2):
+                c = LATTICE[i][d]
+                if c:
+                    along = jnp.where(here, along + v[d] if c == 1 else along - v[d], along)
+        zpack[side(sign)] = zpack[side(sign)] + edge_share[sign] * base * (
+            rest + (4.5 * along + 3.0) * along
+        )
+    for sign in (1, -1):
+        v, rest = solid_velocity(iv[line_of[sign], :])
+        share = state[5, line_of[sign], :]
+        for entry, i in enumerate(LEAVING[1, sign]):
+            along = dot(LATTICE[i], v)
+            ypack[side(sign), entry] = ypack[side(sign), entry] + share * F32(WEIGHTS[i]) * (
+                rest + (4.5 * along + 3.0) * along
+            )
+    for vector in HALOS:
+        if vector[2] != 0 or vector[1] != 0:
+            when_there(vector, lambda vector=vector: halo_copy(vector).start())
+
+    def collide_solid(r):
+        rows = pl.ds(pl.multiple_of(r * 8, 8), 8)
+        v, rest = solid_velocity(iv[rows, :])
+        share = state[5, rows, :]
+        scaled = {w: w * share for w in sorted(set(WEIGHTS))}
+        rel[PLACE[0], rows, :] = rel[PLACE[0], rows, :] + scaled[WEIGHTS[0]] * rest
+        for i in range(1, 19, 2):
+            j = OPPOSITE[i]
+            ps = dot(LATTICE[i], v)
+            even = scaled[WEIGHTS[i]] * (rest + 4.5 * ps * ps)
+            odd = scaled[WEIGHTS[i]] * (3.0 * ps)
+            rel[PLACE[i], rows, :] = rel[PLACE[i], rows, :] + (even + odd)
+            rel[PLACE[j], rows, :] = rel[PLACE[j], rows, :] + (even - odd)
+
+    for x in sorted({0, X - 1}):
+        for h in range(halves):
+            collide_solid(x * halves + h)
     for vector in HALOS:
         if vector[1] == 0 and vector[2] == 0:
-            when_there(vector, lambda vector=vector: halo_copy(vector).start())
-    for sign in (1, -1):
-        for entry, i in enumerate(LEAVING[1, sign]):
-            first = Y - 1 if sign == 1 else 0
-            ypack[side(sign), entry] = rel[PLACE[i], pl.ds(first, X, stride=Y), :]
-    for vector in HALOS:
-        if vector[1] != 0 and vector[2] == 0:
-            when_there(vector, lambda vector=vector: halo_copy(vector).start())
-    for sign in (1, -1):
-        edge = Z - 1 if sign == 1 else 0
-        packed = jnp.zeros((8, Z), F32)
-        for entry, i in enumerate(LEAVING[2, sign]):
-            for r in range(chunks):
-                column = entry * chunks + r
-                turned = rel[PLACE[i], r * 8 : r * 8 + 8, :]
-                if (column - edge) % Z:
-                    turned = pltpu.roll(turned, (column - edge) % Z, 1)
-                packed = jnp.where(lane8 == column, turned, packed)
-        zpack[side(sign)] = packed
-    for vector in HALOS:
-        if vector[2] != 0:
             when_there(vector, lambda vector=vector: halo_copy(vector).start())
 
     own = [recs[13, d] for d in range(6)]
@@ -428,7 +520,7 @@
         for d in range(3):
             contact[d] = contact[d] + jnp.sum(apart[d] * strength, axis=0, keepdims=True)
 
-    each_neighbour(lambda o, v: force_copy(26 - o, tuple(-s for s in v)).wait_recv())
+    wait_all(nearby, frecv, f_sem.at[1])
     force = fsend[13]
     for o in range(27):
         if o != 13:
@@ -454,8 +546,8 @@
 
     def move_copy(n):
         return pltpu.make_async_remote_copy(
-            src_ref=msend.at[n], dst_ref=mrecv.at[n], send_sem=m_send.at[n],
-            recv_sem=m_recv.at[n], device_id=device(FACES[n]), device_id_type=MESH,
+            src_ref=msend.at[n], dst_ref=mrecv.at[n], send_sem=m_sem.at[0],
+            recv_sem=m_sem.at[1], device_id=device(FACES[n]), device_id_type=MESH,
         )
 
     for n, vector in enumerate(FACES):
@@ -463,22 +555,27 @@
         when_there(vector, lambda n=n: move_copy(n).start())
     stay = routed(6, (0, 0, 0))
 
-    each_neighbour(lambda o, v: record_copy(o, v).wait_send())
-    each_neighbour(lambda o, v: force_copy(o, v).wait_send())
-    for vector in HALOS:
-        when_there(vector, lambda vector=vector: halo_copy(vector).wait_send())
-    for vector in HALOS:
-        back = tuple(-step for step in vector)
-        when_there(back, lambda vector=vector: halo_copy(vector).wait_recv())
-    for n, vector in enumerate(FACES):
-        back = tuple(-step for step in vector)
-        when_there(back, lambda n=n: move_copy(n).wait_recv())
+    def collide_rest(step, carry):
+        for n in range(COLLIDE_UNROLL):
+            collide_solid(halves + step * COLLIDE_UNROLL + n)
+        return carry
+
+    lax.fori_loop(0, (X - 2) * halves // COLLIDE_UNROLL, collide_rest, 0)
+
+    wait_all(nearby, recs, a_sem.at[0])
+    wait_all(nearby, fsend, f_sem.at[0])
+    wait_all(lambda n: n[0], xhalo, h_send.at[0])
+    wait_all(lambda n: n[1], yhalo, h_send.at[1])
+    wait_all(tiles_near, thalo, h_send.at[2])
+    wait_all(faces_near, msend, m_sem.at[0])
+    wait_all(faces_near, mrecv, m_sem.at[1])
     for n in range(len(FACES)):
         stay = stay + mrecv[n]
     for d in range(6):
         moved[d] = stay[d : d + 1]
-    for n, vector in enumerate(FACES):
-        when_there(vector, lambda n=n: move_copy(n).wait_send())
+    wait_all(lambda n: n[0], xhalo, h_recv.at[0])
+    wait_all(lambda n: n[1], yhalo, h_recv.at[1])
+    wait_all(tiles_near, thalo, h_recv.at[2])
 
 
 def pass_kernel(sizes, shape, rel, xhalo, yhalo, thalo, moved, out_hbm, part_out, pv, out_sem):
@@ -486,7 +583,7 @@
     chunks = X * Y // 8
     halves = Y // 8
     me = tuple(lax.axis_index(a) for a in ("gx", "gy", "gz"))
-    part_copy = pltpu.make_async_copy(moved, part_out, out_sem.at[len(LATTICE)])
+    part_copy = pltpu.make_async_copy(moved, part_out, out_sem.at[1])
     part_copy.start()
     suby = lax.broadcasted_iota(I32, (Y, Z), 0)
     laney = lax.broadcasted_iota(I32, (Y, Z), 1)
@@ -508,8 +605,6 @@
             other = laney != blocked
             mask = other if mask is None else mask & other
         return mask
-
-    out_copies = [part_copy]
 
     for i in PASS_ORDER:
         c = LATTICE[i]
@@ -560,12 +655,10 @@
                 closed = jnp.broadcast_to(open_back[0, c[0]].astype(I32), (Y, Z))
                 slab = jnp.where(closed > 0, slab, mirror)
             pv[i, x * Y : (x + 1) * Y, :] = slab
-        copy = pltpu.make_async_copy(pv.at[i], out_hbm.at[i], out_sem.at[i])
-        copy.start()
-        out_copies.append(copy)
-
-    for copy in out_copies:
-        copy.wait()
+        pltpu.make_async_copy(pv.at[i], out_hbm.at[i], out_sem.at[0]).start()
+
+    part_copy.wait()
+    pltpu.make_async_copy(pv, out_hbm, out_sem.at[0]).wait()
 
 
 def body(sizes, populations, solid_fraction, intersection, touch, particles, contacts, dest_code, dest_slot):
@@ -606,23 +699,20 @@
             pltpu.VMEM((1, slots), I32),
             pltpu.VMEM((1, slots), I32),
             pltpu.VMEM((27, 6, 1, slots), F32),
-            pltpu.VMEM((5, X * Y, Z), F32),
+            pltpu.VMEM((6, X * Y, Z), F32),
             pltpu.VMEM((4 * LO, Z), F32),
-            pltpu.VMEM((27, 8, slots), F32),
-            pltpu.VMEM((27, 8, slots), F32),
+            pltpu.VMEM((27, 4, slots), F32),
+            pltpu.VMEM((27, 4, slots), F32),
             pltpu.VMEM((2, 5, X, Z), F32),
             pltpu.VMEM((2, 8, Z), F32),
             pltpu.VMEM((len(FACES), 8, slots), F32),
             pltpu.VMEM((len(FACES), 8, slots), F32),
-            dma((8,)),
-            dma((27,)),
-            dma((27,)),
-            dma((27,)),
-            dma((27,)),
-            dma((len(HALOS),)),
-            dma((len(HALOS),)),
-            dma((len(FACES),)),
-            dma((len(FACES),)),
+            dma((7 + X * Y // (8 * SUM_UNROLL),)),
+            dma((2,)),
+            dma((2,)),
+            dma((3,)),
+            dma((3,)),
+            dma((2,)),
         ],
         compiler_params=pltpu.CompilerParams(
             collective_id=0, has_side_effects=True, vmem_limit_bytes=GRANT
@@ -636,7 +726,7 @@
         ),
         in_specs=[vmem] * 5,
         out_specs=(any_space, any_space),
-        scratch_shapes=[pltpu.VMEM((count, X * Y, Z), F32), dma((count + 1,))],
+        scratch_shapes=[pltpu.VMEM((count, X * Y, Z), F32), dma((2,))],
         compiler_params=pltpu.CompilerParams(vmem_limit_bytes=GRANT),
     )(*[pltpu.with_memory_space_constraint(value, pltpu.VMEM) for value in handed])
     return (out.reshape(count, X, Y, Z), moved.reshape(1, 1, 1, 6, slots))

time: 17 us -> 14.1 us (0.83)
  Pallas kernels: 16.2 us -> 13.4 us
    pallas_call x1, Pallas kernels: 14.9 us -> 12.2 us  [body(): pl.pallas_call(functools.partial(kernel, sizes, (X, Y, Z)), out_shape=(pl...]
where the time goes in v1:
time: 14.1 us; the launch traced here: 14 us
  Pallas kernels  13.4 us (95%)
  between operations  0.64 us (5%)
    pallas_call x1, Pallas kernels, body(): pl.pallas_call(functools.partial(kernel, sizes, (X, Y, Z)), out_shape=(pl...  12.2 us
    pallas_call x1, Pallas kernels, body(): pl.pallas_call(functools.partial(pass_kernel, sizes, (X, Y, Z)), out_shap...  1.13 us

profile of v1, /device:TPU:0, one launch (start us, length us, event | category | flops | bytes accessed | tf_op | source)
XLA Modules:
  0.0 14.0 jit_solution(11560296958746483633)
XLA Ops:
  0.6 12.2 %shard_map.95 = (f32[19,128,128]{2,1,0:T(8,128)S(1)}, f32[2,5,16,128]{3,2,1,0:T(8,128)S(1)}, f32[2,5,8,128]{3,2,1,0:T(8,128)S(1)}, f32[14,8,128]{2,1,0:T(8,128)S(1)}, f32[6,1,128]{2,1,0:T(1,128)S(1)}) custom-call(f32[19,128,128]{2,1,0:T(8,128)} %bitcast.12, f32[128,128]{1,0:T(8,128)} %bitcast.13, s32[128,128]{1,0:T(8,128)} %bitcast.14, s32[1,256]{1,0:T(1,128)} %bitcast.17, ...), custom_call_target="tpu_custom_call" | custom-call | tf_op jit(solution)/shard_map/pallas_call | solution.py:682
  12.9 1.1 %shard_map.96 = (f32[19,128,128]{2,1,0:T(8,128)}, f32[6,1,128]{2,1,0:T(1,128)}) custom-call(f32[19,128,128]{2,1,0:T(8,128)S(1)} %get-tuple-element.9.rel, f32[2,5,16,128]{3,2,1,0:T(8,128)S(1)} %get-tuple-element.10.xhalo, f32[2,5,8,128]{3,2,1,0:T(8,128)S(1)} %get-tuple-element.11.yhalo, f32[14,8,128]{2,1,0:T(8,128)S(1)} %get-tuple-element.12.thalo, ...), custom_call_target="tpu_custom_call" | custom-call | tf_op jit(solution)/shard_map/pallas_call | solution.py:721

commit v2 on v1

--- a/solution.py
+++ b/solution.py
@@ -59,9 +59,16 @@
 FACES = [(1, 0, 0), (-1, 0, 0), (0, 1, 0), (0, -1, 0), (0, 0, 1), (0, 0, -1)]
 LO = 8
 GRANT = 16 * 2**20
-SUM_UNROLL = 4
-EARLY_STEPS = 2
+SUM_UNROLL = 8
+EARLY_STEPS = 1
 COLLIDE_UNROLL = 2
+SOLID_UNROLL = 6
+BEYOND = (1, 1, 1)
+BEFORE = (-1, -1, -1)
+
+
+def block_id(vector):
+    return 9 * (vector[0] + 1) + 3 * (vector[1] + 1) + vector[2] + 1
 
 
 def side(sign):
@@ -88,7 +95,7 @@
     rel, xhalo, yhalo, thalo, moved,
     pv, fv, iv, tv, cv, codev, slotv,
     recs, state, sums, fsend, frecv, ypack, zpack, msend, mrecv,
-    in_sem, a_sem, f_sem, h_send, h_recv, m_sem,
+    picked, ruler, in_sem, sent, recs_in, forces_in, edges_in, ready,
 ):
     X, Y, Z = shape
     slots = recs.shape[3]
@@ -98,23 +105,28 @@
     halves = Y // 8
     me = tuple(lax.axis_index(a) for a in ("gx", "gy", "gz"))
 
-    own_in = pltpu.make_async_copy(part_hbm, recs.at[13], in_sem.at[0])
     cell_ins = [
         pltpu.make_async_copy(inter_hbm, iv, in_sem.at[1]),
-        pltpu.make_async_copy(frac_hbm, fv, in_sem.at[2]),
+        pltpu.make_async_copy(frac_hbm, fv, in_sem.at[1]),
     ]
     small_ins = [
-        pltpu.make_async_copy(src, dst, in_sem.at[3 + n])
-        for n, (src, dst) in enumerate(
-            [(touch_hbm, tv), (cont_hbm, cv), (code_hbm, codev), (slot_hbm, slotv)]
-        )
+        pltpu.make_async_copy(src, dst, in_sem.at[0])
+        for src, dst in [
+            (part_hbm, recs.at[13]), (touch_hbm, tv), (cont_hbm, cv), (code_hbm, codev),
+            (slot_hbm, slotv),
+        ]
     ]
+    small_rows = (touches + (neighbours + 8) * slots) // Z
+    cells_done = pltpu.make_async_copy(pops_hbm.at[0:2], pv.at[0:2], in_sem.at[1])
+    small_done = pltpu.make_async_copy(
+        pops_hbm.at[0, 0:small_rows], pv.at[0, 0:small_rows], in_sem.at[0]
+    )
     steps = chunks // SUM_UNROLL
     span = SUM_UNROLL * 8
 
     def pops_in(step):
         rows = pl.ds(pl.multiple_of(step * span, span), span)
-        return pltpu.make_async_copy(pops_hbm.at[:, rows], pv.at[:, rows], in_sem.at[7 + step])
+        return pltpu.make_async_copy(pops_hbm.at[:, rows], pv.at[:, rows], in_sem.at[2 + step])
 
     there = {
         (axis, sign): (me[axis] < sizes[axis] - 1) if sign == 1 else (me[axis] > 0)
@@ -129,46 +141,108 @@
     def device(vector):
         return tuple(position + step for position, step in zip(me, vector))
 
-    def each_neighbour(action):
-        for o in range(27):
-            if o != 13:
-                vector = (o // 9 - 1, (o // 3) % 3 - 1, o % 3 - 1)
-                pl.when(exists(vector))(functools.partial(action, o, vector))
-
-    own_in.start()
+    def steps_along(axis):
+        if sizes[axis] == 1:
+            return [((0,), None)]
+        if sizes[axis] == 2:
+            return [((0, 1 - 2 * me[axis]), None)]
+        return [((-1,), there[axis, -1]), ((0,), None), ((1,), there[axis, 1])]
+
+    def far(vector):
+        return sum(1 for step in vector if not (isinstance(step, int) and step == 0))
+
+    def each_neighbour(action, skip=(2, 2, 2), allow={}, levels=(-1, 0, 1)):
+        groups = []
+        for choice in itertools.product(*[steps_along(axis) for axis in range(3)]):
+            level = choice[2][0][0]
+            if sizes[2] > 2 and level not in levels:
+                continue
+            flags = [flag for _, flag in choice if flag is not None]
+            if level in allow:
+                flags.append(allow[level])
+            vectors = list(itertools.product(*[values for values, _ in choice]))
+            groups.append((flags, sorted([v for v in vectors if far(v)], key=far, reverse=True)))
+
+        def act(vectors):
+            for vector in vectors:
+                do = functools.partial(action, block_id(vector), vector)
+                pairs = list(zip(range(3), vector, skip))
+                fixed = [p for p in pairs if isinstance(p[1], int)]
+                moving = [p for p in pairs if not isinstance(p[1], int)]
+                if any(step != other for _, step, other in fixed) or 2 in skip:
+                    do()
+                elif moving and all(other for _, _, other in moving):
+                    apart = [jnp.logical_not(there[axis, other]) for axis, _, other in moving]
+                    pl.when(functools.reduce(lambda p, q: p | q, apart))(do)
+                elif moving:
+                    do()
+
+        for flags, vectors in sorted(groups, key=lambda g: max(map(far, g[1]), default=0), reverse=True):
+            run = functools.partial(act, vectors)
+            if flags:
+                pl.when(functools.reduce(lambda p, q: p & q, flags))(run)
+            else:
+                run()
+
+    windows = [
+        [0] if size == 1 else [0 - at, 1 - at] if size == 2 else [-1, 0, 1]
+        for size, at in zip(sizes, me)
+    ]
+    blocks = [block_id((x, y, z)) for x in windows[0] for y in windows[1] for z in windows[2]]
+
     barrier = pltpu.get_barrier_semaphore()
+
+    half = sizes[2] // 2
+    split = sizes[2] > 2
+    alone_up = there[2, 1] & (me[2] >= half)
+    alone_down = me[2] > half
+    not_up = {1: jnp.logical_not(alone_up)} if split else {}
+    not_down = {-1: jnp.logical_not(alone_down)} if split else {}
 
     def greet(o, vector):
         pl.semaphore_signal(barrier, inc=1, device_id=device(vector), device_id_type=MESH)
 
-    each_neighbour(greet)
+    for copy in small_ins:
+        copy.start()
     for copy in cell_ins:
         copy.start()
     for step in range(steps):
         pops_in(step).start()
-    for copy in small_ins:
-        copy.start()
+    each_neighbour(greet, BEFORE, not_down)
 
     around = [
         (me[axis] > 0).astype(I32) + (me[axis] < sizes[axis] - 1).astype(I32) for axis in range(3)
     ]
     options = [[0] if size == 1 else [1] if size == 2 else [1, 2] for size in sizes]
     nearby = lambda n: (n[0] + 1) * (n[1] + 1) * (n[2] + 1) - 1
-    tiles_near = lambda n: n[2] + n[0] * n[1] + n[0] * n[2] + n[1] * n[2]
-    faces_near = lambda n: n[0] + n[1] + n[2]
-    count = nearby(around)
-
-    def wait_all(measure, ref, semaphore):
+    record_rows = lambda n: 6 * nearby(n)
+    force_rows = lambda n: 4 * nearby(n)
+
+    def edge_rows(n):
+        x, y, z = n
+        tiles = 8 * (z + x * z + x + y + z) + x * y + y * z
+        return 5 * (Y * x + X * y) + tiles
+
+    sent_rows = lambda n: record_rows(n) + force_rows(n) + edge_rows(n)
+
+    plane = (around[0] + 1) * (around[1] + 1)
+    waiting = exists(BEYOND).astype(I32)
+    if split:
+        waiting = jnp.where(alone_up, plane, waiting)
+    count = nearby(around) - waiting
+
+    def wait_rows(measure, semaphore):
         amount = measure(around)
-        for c in sorted({measure(n) for n in itertools.product(*options)}):
-            if c:
-                part = ref.at[pl.ds(0, c)]
-                pl.when(amount == c)(lambda part=part: pltpu.make_async_copy(part, part, semaphore).wait())
+        for rows in sorted({measure(n) for n in itertools.product(*options)}):
+            if rows:
+                part = ruler.at[0:rows]
+                copy = pltpu.make_async_copy(part, part, semaphore.at[0])
+                pl.when(amount == rows)(copy.wait)
 
     def record_copy(o, vector):
         return pltpu.make_async_remote_copy(
-            src_ref=recs.at[13], dst_ref=recs.at[26 - o], send_sem=a_sem.at[0],
-            recv_sem=a_sem.at[1], device_id=device(vector), device_id_type=MESH,
+            src_ref=recs.at[13], dst_ref=recs.at[26 - o], send_sem=sent.at[0],
+            recv_sem=recs_in.at[0], device_id=device(vector), device_id_type=MESH,
         )
 
     sub8 = lax.broadcasted_iota(I32, (8, Z), 0)
@@ -205,17 +279,19 @@
         pieces = [p[0] for p in pairs] + [p[1] for p in pairs]
         high = index // LO if LO & (LO - 1) else lax.shift_right_logical(index, LO.bit_length() - 1)
         low = index - high * LO
+        return pieces, high, low
+
+    def gather_pairs(pieces, high, low):
         left, right = [], []
         for row in range(8):
             high_row = jnp.broadcast_to(high[row : row + 1], (high_count, Z))
-            low_row = jnp.broadcast_to(low[row : row + 1], (8, Z))
+            match = jnp.broadcast_to(low[row : row + 1], (8, Z)) == sub8
             left.append(jnp.where(high_row == sub_high, F32(1.0), F32(0.0)).astype(BF16))
-            match = low_row == sub8
             right.append(
                 jnp.concatenate(
                     [
-                        jnp.where(match, jnp.broadcast_to(p[row : row + 1], (8, Z)), F32(0.0))
-                        for p in pieces
+                        jnp.where(match, jnp.broadcast_to(pieces[p][row : row + 1], (8, Z)), F32(0.0))
+                        for p in range(8)
                     ],
                     axis=0,
                 ).astype(BF16)
@@ -226,82 +302,82 @@
         pops_in(step).wait()
         right, left = [], []
         for n in range(SUM_UNROLL):
-            more_right, more_left = gather_pieces(step * SUM_UNROLL + n)
+            more_right, more_left = gather_pairs(*gather_pieces(step * SUM_UNROLL + n))
             right += more_right
             left += more_left
-        return total + nt_dot(jnp.concatenate(right, axis=1), jnp.concatenate(left, axis=1))
-
-    for copy in cell_ins:
-        copy.wait()
-    total = jnp.zeros((8 * LO, high_count), F32)
-    if EARLY_STEPS:
-        total = lax.fori_loop(0, EARLY_STEPS, gather_sums, total)
-
-    own_in.wait()
-    pl.semaphore_wait(barrier, count)
-    each_neighbour(lambda o, v: record_copy(o, v).start())
-
-    total = lax.fori_loop(EARLY_STEPS, steps, gather_sums, total)
-    for copy in small_ins:
-        copy.wait()
+        return total + nt_dot(jnp.concatenate(left, axis=1), jnp.concatenate(right, axis=1))
+
+    groups = touches // Z
+
+    def spread_sums(total):
+        sums[:, 0 : 8 * LO] = total
+        both = sums[...]
+        both = both + pltpu.roll(both, Z - 4 * LO, 1)
+        lane_high = lax.shift_right_logical(lane8, LO.bit_length() - 1)
+        lane_low = lane8 - lane_high * LO
+        parts = []
+        for g in range(groups):
+            lines = []
+            for q in range(4):
+                line = jnp.zeros((8, Z), F32)
+                for part in range(Z // (8 * LO)):
+                    first_row = g * (Z // LO) + part * 8
+                    taken = lane_take(both[first_row : first_row + 8], q * LO + lane_low)
+                    line = line + jnp.where(sub8 + part * 8 == lane_high, taken, F32(0.0))
+                lines.append(jnp.sum(line, axis=0, keepdims=True))
+            quad = jnp.concatenate(lines, axis=0)
+            first, second = split_pair(quad)
+            parts.append(jnp.concatenate([first, second], axis=0))
+        table = jnp.concatenate(parts, axis=1)
+        block8 = jnp.broadcast_to(touch_block, (8, touches))
+        spread_left = jnp.concatenate(
+            [jnp.where(block8 == o, table, F32(0.0)) for o in blocks], axis=0
+        ).astype(BF16)
+        spread = nt_dot(spread_left, picked[...])
+        for n, o in enumerate(blocks):
+            piece = spread[n * 8 : (n + 1) * 8]
+            fsend[o] = (piece + pltpu.roll(piece, 4, 0))[0:4]
+
+    middle = (lax.rem(me[0], 2) == 1) & there[0, 1]
+    idle = (there[1, 1] & there[2, 1]) | (middle & (there[1, 1] | there[2, 1]))
+    if split:
+        idle = idle & ((me[2] < half) | middle)
+    first_steps = jnp.where(idle, steps, EARLY_STEPS)
+    if split:
+        late = (me[2] >= half) & jnp.logical_not(idle)
+        first_steps = jnp.where(late & jnp.logical_not(there[1, 1]), 0, first_steps)
     sums[...] = jnp.zeros(sums.shape, F32)
-    sums[:, 0:high_count] = total[0 : 4 * LO] + total[4 * LO : 8 * LO]
-
-    groups = touches // Z
-    parts = []
-    for g in range(groups):
-        k = lane8 + g * Z
-        k_high = lax.shift_right_logical(k, LO.bit_length() - 1)
-        k_low = k - k_high * LO
-        lines = []
-        for q in range(4):
-            taken = lane_take(sums[q * LO : (q + 1) * LO, :], k_high)
-            lines.append(jnp.sum(jnp.where(k_low == sub8, taken, F32(0.0)), axis=0, keepdims=True))
-        quad = jnp.concatenate(lines, axis=0)
-        first, second = split_pair(quad)
-        parts.append(jnp.concatenate([first, second], axis=0))
-    table = jnp.concatenate(parts, axis=1)
+    frecv[13] = jnp.zeros(frecv.shape[1:], F32)
+
+    def clear(ids):
+        for o in ids:
+            recs[o] = jnp.zeros(recs.shape[1:], F32)
+            frecv[o] = jnp.zeros(frecv.shape[1:], F32)
+
+    for choice in itertools.product(*[steps_along(axis) for axis in range(3)]):
+        flags = [flag for _, flag in choice if flag is not None]
+        if flags:
+            ids = [block_id(vector) for vector in itertools.product(*[values for values, _ in choice])]
+            present = functools.reduce(lambda p, q: p & q, flags)
+            pl.when(jnp.logical_not(present))(functools.partial(clear, ids))
+    for n, vector in enumerate(FACES):
+        back = tuple(-step for step in vector)
+
+        def clear_moved(n=n):
+            mrecv[n] = jnp.zeros(mrecv.shape[1:], F32)
+
+        pl.when(jnp.logical_not(exists(back)))(clear_moved)
+
+    small_done.wait()
     touch_row = tv[...]
     touch_block = lax.shift_right_logical(touch_row, slots.bit_length() - 1)
     touch_slot = touch_row - touch_block * slots
-    block8 = jnp.broadcast_to(touch_block, (8, touches))
-    spread_left = jnp.concatenate(
-        [jnp.where(block8 == o, table, F32(0.0)) for o in range(27)], axis=0
-    ).astype(BF16)
-    pick = jnp.where(
+    picked[...] = jnp.where(
         jnp.broadcast_to(touch_slot, (slots, touches))
         == lax.broadcasted_iota(I32, (slots, touches), 0),
         F32(1.0),
         F32(0.0),
     ).astype(BF16)
-    spread = nt_dot(spread_left, pick)
-    for o in range(27):
-        piece = spread[o * 8 : (o + 1) * 8]
-        fsend[o] = (piece + pltpu.roll(piece, 4, 0))[0:4]
-
-    def force_copy(o, vector):
-        return pltpu.make_async_remote_copy(
-            src_ref=fsend.at[o], dst_ref=frecv.at[26 - o], send_sem=f_sem.at[0],
-            recv_sem=f_sem.at[1], device_id=device(vector), device_id_type=MESH,
-        )
-
-    each_neighbour(lambda o, v: force_copy(o, v).start())
-
-    def clear(o):
-        recs[o] = jnp.zeros(recs.shape[1:], F32)
-        frecv[o] = jnp.zeros(frecv.shape[1:], F32)
-
-    for o in range(27):
-        if o != 13:
-            vector = (o // 9 - 1, (o // 3) % 3 - 1, o % 3 - 1)
-            pl.when(jnp.logical_not(exists(vector)))(functools.partial(clear, o))
-    for n, vector in enumerate(FACES):
-        back = tuple(-step for step in vector)
-
-        def clear_moved(n=n):
-            mrecv[n] = jnp.zeros(mrecv.shape[1:], F32)
-
-        pl.when(jnp.logical_not(exists(back)))(clear_moved)
 
     code = codev[...]
     wanted_codes = [9 * (v[0] + 1) + 3 * (v[1] + 1) + v[2] + 1 for v in FACES] + [13]
@@ -317,6 +393,33 @@
         F32(0.0),
     ).astype(BF16)
     taken_from = nt_dot(route, place).astype(I32)
+
+    cells_done.wait()
+    total = lax.fori_loop(0, first_steps, gather_sums, jnp.zeros((high_count, 8 * LO), F32))
+    pl.when(idle)(lambda: spread_sums(total))
+
+    pl.semaphore_wait(barrier, count)
+    def answer(o, vector):
+        pl.semaphore_signal(ready.at[0], inc=1, device_id=device(vector), device_id_type=MESH)
+
+    answer_far = functools.partial(answer, block_id(BEFORE), BEFORE)
+    if split:
+        pl.when(alone_down)(lambda: each_neighbour(answer, levels=(-1,)))
+        pl.when(exists(BEFORE) & jnp.logical_not(alone_down))(answer_far)
+    else:
+        pl.when(exists(BEFORE))(answer_far)
+    each_neighbour(lambda o, v: record_copy(o, v).start(), BEYOND, not_up)
+
+    total = lax.fori_loop(first_steps, steps, gather_sums, total)
+    pl.when(jnp.logical_not(idle))(lambda: spread_sums(total))
+
+    def force_copy(o, vector):
+        return pltpu.make_async_remote_copy(
+            src_ref=fsend.at[o], dst_ref=frecv.at[26 - o], send_sem=sent.at[0],
+            recv_sem=forces_in.at[0], device_id=device(vector), device_id_type=MESH,
+        )
+
+    each_neighbour(lambda o, v: force_copy(o, v).start(), BEYOND, not_up)
 
     def dot(c, vec):
         value = None
@@ -389,27 +492,40 @@
         edge_share[sign] = lane_take(share, repeat)
         edge_index[sign] = lane_take(index, repeat)
 
-    wait_all(nearby, recs, a_sem.at[1])
+    def reach_far():
+        pl.semaphore_wait(ready.at[0], 1)
+        record_copy(block_id(BEYOND), BEYOND).start()
+        force_copy(block_id(BEYOND), BEYOND).start()
+
+    def reach_up():
+        pl.semaphore_wait(ready.at[0], plane)
+        each_neighbour(lambda o, v: record_copy(o, v).start(), levels=(1,))
+        each_neighbour(lambda o, v: force_copy(o, v).start(), levels=(1,))
+
+    if split:
+        pl.when(alone_up)(reach_up)
+        pl.when(exists(BEYOND) & jnp.logical_not(alone_up))(reach_far)
+    else:
+        pl.when(exists(BEYOND))(reach_far)
+    wait_rows(record_rows, recs_in)
+
+    def place_of(index):
+        block = lax.shift_right_logical(index, slots.bit_length() - 1)
+        return block, index - block * slots
+
+    def wide(o, row):
+        return jnp.broadcast_to(recs[o, row], (8, Z))
 
     index_rows = [touch_row[:, g * Z : (g + 1) * Z] for g in range(groups)]
-    touch8 = jnp.concatenate(
-        index_rows + [jnp.full((8 - groups, Z), 27 * slots, I32)], axis=0
-    )
-
-    def fetch(first_row, index):
-        found = [jnp.zeros((8, Z), F32)] * 3
-        block = lax.shift_right_logical(index, slots.bit_length() - 1)
-        local = index - block * slots
-        for o in range(27):
-            hit = block == o
-            for d in range(3):
-                row = jnp.broadcast_to(recs[o, first_row + d], (8, Z))
-                found[d] = jnp.where(hit, lane_take(row, local), found[d])
-        return found
-
-    touch_velocity = [SPEED_UNIT * v for v in fetch(3, touch8)]
+    unused = [jnp.full((8 - 3 * groups, Z), 27 * slots, I32)] if groups * 3 < 8 else []
+    touch_blocks, touch_local = place_of(jnp.concatenate(index_rows * 3 + unused, axis=0))
+    found = jnp.zeros((8, Z), F32)
+    for o in blocks:
+        rows = jnp.where(sub8 < groups, wide(o, 3), jnp.where(sub8 < 2 * groups, wide(o, 4), wide(o, 5)))
+        found = jnp.where(touch_blocks == o, lane_take(rows, touch_local), found)
+    found = SPEED_UNIT * found
     tables = [
-        [jnp.broadcast_to(touch_velocity[d][g : g + 1], (8, Z)) for g in range(groups)]
+        [jnp.broadcast_to(found[d * groups + g][None], (8, Z)) for g in range(groups)]
         for d in range(3)
     ]
 
@@ -425,12 +541,15 @@
         return v, 1.0 - 1.5 * (v[0] * v[0] + v[1] * v[1] + v[2] * v[2])
 
     def halo_copy(vector):
-        m = 2 if vector[2] != 0 or (vector[0] != 0 and vector[1] != 0) else 0 if vector[0] != 0 else 1
-        if vector[2] != 0:
+        if vector[2] != 0 and vector[1] != 0:
+            row = pl.ds((Y - 1) % 8 if vector[1] == 1 else 0, 1)
+            src, dst = zpack.at[side(vector[2]), row], thalo.at[TILE_ID[vector], row]
+        elif vector[2] != 0:
             src, dst = zpack.at[side(vector[2])], thalo.at[TILE_ID[vector]]
         elif vector[0] != 0 and vector[1] != 0:
             entry = LEAVING[1, vector[1]].index(LATTICE.index(vector))
-            src, dst = ypack.at[side(vector[1]), entry], thalo.at[TILE_ID[vector]]
+            row = pl.ds(X - 1 if vector[0] == 1 else 0, 1)
+            src, dst = ypack.at[side(vector[1]), entry, row], thalo.at[TILE_ID[vector], row]
         elif vector[0] != 0:
             start = 5 * side(vector[0])
             row = (X - 1) * Y if vector[0] == 1 else 0
@@ -439,7 +558,7 @@
         else:
             src, dst = ypack.at[side(vector[1])], yhalo.at[side(vector[1])]
         return pltpu.make_async_remote_copy(
-            src_ref=src, dst_ref=dst, send_sem=h_send.at[m], recv_sem=h_recv.at[m],
+            src_ref=src, dst_ref=dst, send_sem=sent.at[0], recv_sem=edges_in.at[0],
             device_id=device(vector), device_id_type=MESH,
         )
 
@@ -461,6 +580,9 @@
         zpack[side(sign)] = zpack[side(sign)] + edge_share[sign] * base * (
             rest + (4.5 * along + 3.0) * along
         )
+    for vector in HALOS[::-1]:
+        if vector[2] != 0:
+            when_there(vector, lambda vector=vector: halo_copy(vector).start())
     for sign in (1, -1):
         v, rest = solid_velocity(iv[line_of[sign], :])
         share = state[5, line_of[sign], :]
@@ -469,8 +591,8 @@
             ypack[side(sign), entry] = ypack[side(sign), entry] + share * F32(WEIGHTS[i]) * (
                 rest + (4.5 * along + 3.0) * along
             )
-    for vector in HALOS:
-        if vector[2] != 0 or vector[1] != 0:
+    for vector in HALOS[::-1]:
+        if vector[2] == 0 and vector[1] != 0:
             when_there(vector, lambda vector=vector: halo_copy(vector).start())
 
     def collide_solid(r):
@@ -487,44 +609,52 @@
             rel[PLACE[i], rows, :] = rel[PLACE[i], rows, :] + (even + odd)
             rel[PLACE[j], rows, :] = rel[PLACE[j], rows, :] + (even - odd)
 
-    for x in sorted({0, X - 1}):
-        for h in range(halves):
-            collide_solid(x * halves + h)
-    for vector in HALOS:
-        if vector[1] == 0 and vector[2] == 0:
-            when_there(vector, lambda vector=vector: halo_copy(vector).start())
-
     own = [recs[13, d] for d in range(6)]
     contact = [jnp.zeros((1, slots), F32) for _ in range(3)]
     spans = (X / R, Y / R, Z / R)
     for start in range(0, neighbours, 8):
-        stop = min(start + 8, neighbours)
-        lines = [cv[n] for n in range(start, stop)]
-        if stop - start < 8:
-            lines.append(jnp.full((8 - stop + start, slots), 27 * slots, I32))
+        used = min(8, neighbours - start)
+        lines = [cv[n] for n in range(start, start + used)]
+        half = used <= 4
+        if half:
+            lines = (lines + [jnp.full((4 - used, slots), 27 * slots, I32)] * (used < 4)) * 2
+        elif used < 8:
+            lines.append(jnp.full((8 - used, slots), 27 * slots, I32))
         entries = jnp.concatenate(lines, axis=0)
-        found = fetch(0, entries)
-        block = lax.shift_right_logical(entries, slots.bit_length() - 1)
-        nine = jnp.zeros(block.shape, I32)
+        entry_block, local = place_of(entries)
+        near = [jnp.zeros((8, slots), F32)] * (2 if half else 3)
+        for o in blocks:
+            hit = entry_block == o
+            lines = [wide(o, d) for d in range(3)]
+            if half:
+                lines = [jnp.where(sub8 < 4, lines[0], lines[1]), lines[2]]
+            near = [
+                jnp.where(hit, lane_take(line, local), value) for line, value in zip(lines, near)
+            ]
+        if half:
+            near = [near[0], pltpu.roll(near[0], 4, 0), near[1]]
+        nine = jnp.zeros(entry_block.shape, I32)
         for step in (9, 18, 27):
-            nine = nine + (block >= step).astype(I32)
-        inner = block - 9 * nine
+            nine = nine + (entry_block >= step).astype(I32)
+        inner = entry_block - 9 * nine
         three = (inner >= 3).astype(I32) + (inner >= 6).astype(I32)
         moves = (nine - 1, three - 1, inner - 3 * three - 1)
         apart = [
-            jnp.broadcast_to(own[d], (8, slots)) - (found[d] + moves[d].astype(F32) * spans[d])
+            jnp.broadcast_to(own[d], (8, slots)) - (near[d] + moves[d].astype(F32) * spans[d])
             for d in range(3)
         ]
         soften = 1.0 + 0.25 * (apart[0] * apart[0] + apart[1] * apart[1] + apart[2] * apart[2])
-        strength = CONTACT_GAIN * (entries < 27 * slots).astype(F32) / (soften * soften)
+        valid = entries < 27 * slots
+        if half:
+            valid = valid & (sub8 < 4)
+        strength = CONTACT_GAIN * valid.astype(F32) / (soften * soften)
         for d in range(3):
             contact[d] = contact[d] + jnp.sum(apart[d] * strength, axis=0, keepdims=True)
 
-    wait_all(nearby, frecv, f_sem.at[1])
+    wait_rows(force_rows, forces_in)
     force = fsend[13]
-    for o in range(27):
-        if o != 13:
-            force = force + frecv[o]
+    for o in blocks:
+        force = force + frecv[o]
     gravity = (0.0, 0.0, GRAVITY_STEP)
     velocity_new, position_new = [], []
     for d in range(3):
@@ -546,8 +676,8 @@
 
     def move_copy(n):
         return pltpu.make_async_remote_copy(
-            src_ref=msend.at[n], dst_ref=mrecv.at[n], send_sem=m_sem.at[0],
-            recv_sem=m_sem.at[1], device_id=device(FACES[n]), device_id_type=MESH,
+            src_ref=msend.at[n], dst_ref=mrecv.at[n], send_sem=sent.at[0],
+            recv_sem=edges_in.at[0], device_id=device(FACES[n]), device_id_type=MESH,
         )
 
     for n, vector in enumerate(FACES):
@@ -555,27 +685,26 @@
         when_there(vector, lambda n=n: move_copy(n).start())
     stay = routed(6, (0, 0, 0))
 
+    for x in sorted({0, X - 1}):
+        for h in range(halves):
+            collide_solid(x * halves + h)
+    for vector in HALOS:
+        if vector[1] == 0 and vector[2] == 0:
+            when_there(vector, lambda vector=vector: halo_copy(vector).start())
+
     def collide_rest(step, carry):
-        for n in range(COLLIDE_UNROLL):
-            collide_solid(halves + step * COLLIDE_UNROLL + n)
+        for n in range(SOLID_UNROLL):
+            collide_solid(halves + step * SOLID_UNROLL + n)
         return carry
 
-    lax.fori_loop(0, (X - 2) * halves // COLLIDE_UNROLL, collide_rest, 0)
-
-    wait_all(nearby, recs, a_sem.at[0])
-    wait_all(nearby, fsend, f_sem.at[0])
-    wait_all(lambda n: n[0], xhalo, h_send.at[0])
-    wait_all(lambda n: n[1], yhalo, h_send.at[1])
-    wait_all(tiles_near, thalo, h_send.at[2])
-    wait_all(faces_near, msend, m_sem.at[0])
-    wait_all(faces_near, mrecv, m_sem.at[1])
+    lax.fori_loop(0, (X - 2) * halves // SOLID_UNROLL, collide_rest, 0)
+
+    wait_rows(sent_rows, sent)
+    wait_rows(edge_rows, edges_in)
     for n in range(len(FACES)):
         stay = stay + mrecv[n]
     for d in range(6):
         moved[d] = stay[d : d + 1]
-    wait_all(lambda n: n[0], xhalo, h_recv.at[0])
-    wait_all(lambda n: n[1], yhalo, h_recv.at[1])
-    wait_all(tiles_near, thalo, h_recv.at[2])
 
 
 def pass_kernel(sizes, shape, rel, xhalo, yhalo, thalo, moved, out_hbm, part_out, pv, out_sem):
@@ -700,19 +829,21 @@
             pltpu.VMEM((1, slots), I32),
             pltpu.VMEM((27, 6, 1, slots), F32),
             pltpu.VMEM((6, X * Y, Z), F32),
-            pltpu.VMEM((4 * LO, Z), F32),
+            pltpu.VMEM((touches // LO, Z), F32),
             pltpu.VMEM((27, 4, slots), F32),
             pltpu.VMEM((27, 4, slots), F32),
             pltpu.VMEM((2, 5, X, Z), F32),
             pltpu.VMEM((2, 8, Z), F32),
             pltpu.VMEM((len(FACES), 8, slots), F32),
             pltpu.VMEM((len(FACES), 8, slots), F32),
-            dma((7 + X * Y // (8 * SUM_UNROLL),)),
-            dma((2,)),
-            dma((2,)),
-            dma((3,)),
-            dma((3,)),
-            dma((2,)),
+            pltpu.VMEM((slots, touches), BF16),
+            pltpu.VMEM((26 * 10 + 10 * (X + Y) + 8 * (len(TILES) + len(FACES)), Z), F32),
+            dma((2 + X * Y // (8 * SUM_UNROLL),)),
+            dma((1,)),
+            dma((1,)),
+            dma((1,)),
+            dma((1,)),
+            pltpu.SemaphoreType.REGULAR((1,)),
         ],
         compiler_params=pltpu.CompilerParams(
             collective_id=0, has_side_effects=True, vmem_limit_bytes=GRANT

time: 14.1 us -> 13.4 us (0.950)
  Pallas kernels: 13.4 us -> 12.6 us
    pallas_call x1, Pallas kernels: 12.2 us -> 11.5 us  [body(): pl.pallas_call(functools.partial(kernel, sizes, (X, Y, Z)), out_shape=(pl...]
where the time goes in v2:
time: 13.4 us; the launch traced here: 13.2 us
  Pallas kernels  12.6 us (94%)
  between operations  0.64 us (5%)
    pallas_call x1, Pallas kernels, body(): pl.pallas_call(functools.partial(kernel, sizes, (X, Y, Z)), out_shape=(pl...  11.5 us
    pallas_call x1, Pallas kernels, body(): pl.pallas_call(functools.partial(pass_kernel, sizes, (X, Y, Z)), out_shap...  1.13 us

profile of v2, /device:TPU:0, one launch (start us, length us, event | category | flops | bytes accessed | tf_op | source)
XLA Modules:
  0.0 13.2 jit_solution(11857668253888276402)
XLA Ops:
  0.6 11.5 %shard_map.95 = (f32[19,128,128]{2,1,0:T(8,128)S(1)}, f32[2,5,16,128]{3,2,1,0:T(8,128)S(1)}, f32[2,5,8,128]{3,2,1,0:T(8,128)S(1)}, f32[14,8,128]{2,1,0:T(8,128)S(1)}, f32[6,1,128]{2,1,0:T(1,128)S(1)}) custom-call(f32[19,128,128]{2,1,0:T(8,128)} %bitcast.12, f32[128,128]{1,0:T(8,128)} %bitcast.13, s32[128,128]{1,0:T(8,128)} %bitcast.14, s32[1,256]{1,0:T(1,128)} %bitcast.17, ...), custom_call_target="tpu_custom_call" | custom-call | tf_op jit(solution)/shard_map/pallas_call | solution.py:811
  12.1 1.1 %shard_map.96 = (f32[19,128,128]{2,1,0:T(8,128)}, f32[6,1,128]{2,1,0:T(1,128)}) custom-call(f32[19,128,128]{2,1,0:T(8,128)S(1)} %get-tuple-element.9.rel, f32[2,5,16,128]{3,2,1,0:T(8,128)S(1)} %get-tuple-element.10.xhalo, f32[2,5,8,128]{3,2,1,0:T(8,128)S(1)} %get-tuple-element.11.yhalo, f32[14,8,128]{2,1,0:T(8,128)S(1)} %get-tuple-element.12.thalo, ...), custom_call_target="tpu_custom_call" | custom-call | tf_op jit(solution)/shard_map/pallas_call | solution.py:852

commit v3 on v2

--- a/solution.py
+++ b/solution.py
@@ -62,7 +62,7 @@
 SUM_UNROLL = 8
 EARLY_STEPS = 1
 COLLIDE_UNROLL = 2
-SOLID_UNROLL = 6
+SOLID_UNROLL = 8
 BEYOND = (1, 1, 1)
 BEFORE = (-1, -1, -1)
 
@@ -95,7 +95,7 @@
     rel, xhalo, yhalo, thalo, moved,
     pv, fv, iv, tv, cv, codev, slotv,
     recs, state, sums, fsend, frecv, ypack, zpack, msend, mrecv,
-    picked, ruler, in_sem, sent, recs_in, forces_in, edges_in, ready,
+    picked, ruler, xpack, in_sem, sent, recs_in, forces_in, edges_in, ready,
 ):
     X, Y, Z = shape
     slots = recs.shape[3]
@@ -204,9 +204,10 @@
 
     for copy in small_ins:
         copy.start()
+    pops_in(0).start()
     for copy in cell_ins:
         copy.start()
-    for step in range(steps):
+    for step in range(1, steps):
         pops_in(step).start()
     each_neighbour(greet, BEFORE, not_down)
 
@@ -312,7 +313,6 @@
     def spread_sums(total):
         sums[:, 0 : 8 * LO] = total
         both = sums[...]
-        both = both + pltpu.roll(both, Z - 4 * LO, 1)
         lane_high = lax.shift_right_logical(lane8, LO.bit_length() - 1)
         lane_low = lane8 - lane_high * LO
         parts = []
@@ -322,30 +322,40 @@
                 line = jnp.zeros((8, Z), F32)
                 for part in range(Z // (8 * LO)):
                     first_row = g * (Z // LO) + part * 8
-                    taken = lane_take(both[first_row : first_row + 8], q * LO + lane_low)
+                    rows = both[first_row : first_row + 8]
+                    taken = lane_take(rows, q * LO + lane_low)
+                    taken = taken + lane_take(rows, (4 + q) * LO + lane_low)
                     line = line + jnp.where(sub8 + part * 8 == lane_high, taken, F32(0.0))
                 lines.append(jnp.sum(line, axis=0, keepdims=True))
             quad = jnp.concatenate(lines, axis=0)
             first, second = split_pair(quad)
-            parts.append(jnp.concatenate([first, second], axis=0))
-        table = jnp.concatenate(parts, axis=1)
+            parts.append((first, second))
+        tables = [
+            jnp.concatenate([jnp.concatenate([part[h]] * 2, axis=0) for part in parts], axis=1)
+            for h in range(2)
+        ]
         block8 = jnp.broadcast_to(touch_block, (8, touches))
-        spread_left = jnp.concatenate(
-            [jnp.where(block8 == o, table, F32(0.0)) for o in blocks], axis=0
-        ).astype(BF16)
-        spread = nt_dot(spread_left, picked[...])
+        upper = lax.broadcasted_iota(I32, (8, touches), 0) < 4
+        lefts = []
+        for n in range(0, len(blocks), 2):
+            hit = block8 == jnp.where(upper, blocks[n], blocks[min(n + 1, len(blocks) - 1)])
+            lefts.append(
+                jnp.concatenate([jnp.where(hit, table, F32(0.0)) for table in tables], axis=1)
+            )
+        spread = nt_dot(jnp.concatenate(lefts, axis=0).astype(BF16), picked[...])
         for n, o in enumerate(blocks):
-            piece = spread[n * 8 : (n + 1) * 8]
-            fsend[o] = (piece + pltpu.roll(piece, 4, 0))[0:4]
+            fsend[o] = spread[4 * n : 4 * n + 4]
 
     middle = (lax.rem(me[0], 2) == 1) & there[0, 1]
     idle = (there[1, 1] & there[2, 1]) | (middle & (there[1, 1] | there[2, 1]))
     if split:
-        idle = idle & ((me[2] < half) | middle)
+        idle = jnp.where(me[2] < half, idle, middle & there[1, 1])
     first_steps = jnp.where(idle, steps, EARLY_STEPS)
     if split:
-        late = (me[2] >= half) & jnp.logical_not(idle)
-        first_steps = jnp.where(late & jnp.logical_not(there[1, 1]), 0, first_steps)
+        last_y = jnp.logical_not(there[1, 1])
+        top = jnp.logical_not(there[2, 1])
+        first_steps = jnp.where((me[2] >= half) & (last_y | top), 0, first_steps)
+        first_steps = jnp.where((me[2] >= half) & middle, jnp.where(last_y, 1, steps), first_steps)
     sums[...] = jnp.zeros(sums.shape, F32)
     frecv[13] = jnp.zeros(frecv.shape[1:], F32)
 
@@ -372,12 +382,42 @@
     touch_row = tv[...]
     touch_block = lax.shift_right_logical(touch_row, slots.bit_length() - 1)
     touch_slot = touch_row - touch_block * slots
-    picked[...] = jnp.where(
+    chosen = jnp.where(
         jnp.broadcast_to(touch_slot, (slots, touches))
         == lax.broadcasted_iota(I32, (slots, touches), 0),
         F32(1.0),
         F32(0.0),
     ).astype(BF16)
+    picked[:, 0:touches] = chosen
+    picked[:, touches : 2 * touches] = chosen
+
+    pl.when(first_steps > 0)(cells_done.wait)
+    total = lax.fori_loop(0, first_steps, gather_sums, jnp.zeros((high_count, 8 * LO), F32))
+    pl.when(idle)(lambda: spread_sums(total))
+
+    pl.semaphore_wait(barrier, count)
+    def answer(o, vector):
+        pl.semaphore_signal(ready.at[0], inc=1, device_id=device(vector), device_id_type=MESH)
+
+    answer_far = functools.partial(answer, block_id(BEFORE), BEFORE)
+    if split:
+        pl.when(alone_down)(lambda: each_neighbour(answer, levels=(-1,)))
+        pl.when(exists(BEFORE) & jnp.logical_not(alone_down))(answer_far)
+    else:
+        pl.when(exists(BEFORE))(answer_far)
+    each_neighbour(lambda o, v: record_copy(o, v).start(), BEYOND, not_up)
+
+    pl.when(first_steps == 0)(cells_done.wait)
+    total = lax.fori_loop(first_steps, steps, gather_sums, total)
+    pl.when(jnp.logical_not(idle))(lambda: spread_sums(total))
+
+    def force_copy(o, vector):
+        return pltpu.make_async_remote_copy(
+            src_ref=fsend.at[o], dst_ref=frecv.at[26 - o], send_sem=sent.at[0],
+            recv_sem=forces_in.at[0], device_id=device(vector), device_id_type=MESH,
+        )
+
+    each_neighbour(lambda o, v: force_copy(o, v).start(), BEYOND, not_up)
 
     code = codev[...]
     wanted_codes = [9 * (v[0] + 1) + 3 * (v[1] + 1) + v[2] + 1 for v in FACES] + [13]
@@ -393,33 +433,6 @@
         F32(0.0),
     ).astype(BF16)
     taken_from = nt_dot(route, place).astype(I32)
-
-    cells_done.wait()
-    total = lax.fori_loop(0, first_steps, gather_sums, jnp.zeros((high_count, 8 * LO), F32))
-    pl.when(idle)(lambda: spread_sums(total))
-
-    pl.semaphore_wait(barrier, count)
-    def answer(o, vector):
-        pl.semaphore_signal(ready.at[0], inc=1, device_id=device(vector), device_id_type=MESH)
-
-    answer_far = functools.partial(answer, block_id(BEFORE), BEFORE)
-    if split:
-        pl.when(alone_down)(lambda: each_neighbour(answer, levels=(-1,)))
-        pl.when(exists(BEFORE) & jnp.logical_not(alone_down))(answer_far)
-    else:
-        pl.when(exists(BEFORE))(answer_far)
-    each_neighbour(lambda o, v: record_copy(o, v).start(), BEYOND, not_up)
-
-    total = lax.fori_loop(first_steps, steps, gather_sums, total)
-    pl.when(jnp.logical_not(idle))(lambda: spread_sums(total))
-
-    def force_copy(o, vector):
-        return pltpu.make_async_remote_copy(
-            src_ref=fsend.at[o], dst_ref=frecv.at[26 - o], send_sem=sent.at[0],
-            recv_sem=forces_in.at[0], device_id=device(vector), device_id_type=MESH,
-        )
-
-    each_neighbour(lambda o, v: force_copy(o, v).start(), BEYOND, not_up)
 
     def dot(c, vec):
         value = None
@@ -551,10 +564,7 @@
             row = pl.ds(X - 1 if vector[0] == 1 else 0, 1)
             src, dst = ypack.at[side(vector[1]), entry, row], thalo.at[TILE_ID[vector], row]
         elif vector[0] != 0:
-            start = 5 * side(vector[0])
-            row = (X - 1) * Y if vector[0] == 1 else 0
-            src = rel.at[pl.ds(start, 5), pl.ds(row, Y), :]
-            dst = xhalo.at[side(vector[0])]
+            src, dst = xpack.at[side(vector[0])], xhalo.at[side(vector[0])]
         else:
             src, dst = ypack.at[side(vector[1])], yhalo.at[side(vector[1])]
         return pltpu.make_async_remote_copy(
@@ -608,6 +618,24 @@
             odd = scaled[WEIGHTS[i]] * (3.0 * ps)
             rel[PLACE[i], rows, :] = rel[PLACE[i], rows, :] + (even + odd)
             rel[PLACE[j], rows, :] = rel[PLACE[j], rows, :] + (even - odd)
+
+    def x_faces(sign):
+        face = side(sign)
+        for h in range(halves):
+            row = ((X - 1) * Y if sign == 1 else 0) + h * 8
+            rows = pl.ds(row, 8)
+            v, rest = solid_velocity(iv[rows, :])
+            share = state[5, rows, :]
+            for entry, i in enumerate(LEAVING[0, sign]):
+                along = dot(LATTICE[i], v)
+                xpack[face, entry, pl.ds(h * 8, 8)] = rel[PLACE[i], rows, :] + share * F32(
+                    WEIGHTS[i]
+                ) * (rest + (4.5 * along + 3.0) * along)
+        when_there((sign, 0, 0), lambda: halo_copy((sign, 0, 0)).start())
+
+    odd = lax.rem(me[0], 2) == 1
+    pl.when(odd)(lambda: x_faces(1))
+    pl.when(jnp.logical_not(odd))(lambda: x_faces(-1))
 
     own = [recs[13, d] for d in range(6)]
     contact = [jnp.zeros((1, slots), F32) for _ in range(3)]
@@ -652,9 +680,10 @@
             contact[d] = contact[d] + jnp.sum(apart[d] * strength, axis=0, keepdims=True)
 
     wait_rows(force_rows, forces_in)
-    force = fsend[13]
-    for o in blocks:
-        force = force + frecv[o]
+    terms = [fsend[13]] + [frecv[o] for o in blocks]
+    while len(terms) > 1:
+        terms = [sum(terms[n + 1 : n + 2], terms[n]) for n in range(0, len(terms), 2)]
+    force = terms[0]
     gravity = (0.0, 0.0, GRAVITY_STEP)
     velocity_new, position_new = [], []
     for d in range(3):
@@ -682,22 +711,19 @@
 
     for n, vector in enumerate(FACES):
         msend[n] = routed(n, vector)
+    stay = routed(6, (0, 0, 0))
+    for n, vector in reversed(list(enumerate(FACES))):
         when_there(vector, lambda n=n: move_copy(n).start())
-    stay = routed(6, (0, 0, 0))
-
-    for x in sorted({0, X - 1}):
-        for h in range(halves):
-            collide_solid(x * halves + h)
-    for vector in HALOS:
-        if vector[1] == 0 and vector[2] == 0:
-            when_there(vector, lambda vector=vector: halo_copy(vector).start())
+
+    pl.when(odd)(lambda: x_faces(-1))
+    pl.when(jnp.logical_not(odd))(lambda: x_faces(1))
 
     def collide_rest(step, carry):
         for n in range(SOLID_UNROLL):
-            collide_solid(halves + step * SOLID_UNROLL + n)
+            collide_solid(step * SOLID_UNROLL + n)
         return carry
 
-    lax.fori_loop(0, (X - 2) * halves // SOLID_UNROLL, collide_rest, 0)
+    lax.fori_loop(0, chunks // SOLID_UNROLL, collide_rest, 0)
 
     wait_rows(sent_rows, sent)
     wait_rows(edge_rows, edges_in)
@@ -836,8 +862,9 @@
             pltpu.VMEM((2, 8, Z), F32),
             pltpu.VMEM((len(FACES), 8, slots), F32),
             pltpu.VMEM((len(FACES), 8, slots), F32),
-            pltpu.VMEM((slots, touches), BF16),
+            pltpu.VMEM((slots, 2 * touches), BF16),
             pltpu.VMEM((26 * 10 + 10 * (X + Y) + 8 * (len(TILES) + len(FACES)), Z), F32),
+            pltpu.VMEM((2, 5, Y, Z), F32),
             dma((2 + X * Y // (8 * SUM_UNROLL),)),
             dma((1,)),
             dma((1,)),

time: 13.4 us -> 13.3 us (level)
  no operation moved by 1% of the time
where the time goes in v3:
time: 13.3 us; the launch traced here: 13.1 us
  Pallas kernels  12.5 us (94%)
  between operations  0.64 us (5%)
    pallas_call x1, Pallas kernels, body(): pl.pallas_call(functools.partial(kernel, sizes, (X, Y, Z)), out_shape=(pl...  11.3 us
    pallas_call x1, Pallas kernels, body(): pl.pallas_call(functools.partial(pass_kernel, sizes, (X, Y, Z)), out_shap...  1.13 us

profile of v3, /device:TPU:0, one launch (start us, length us, event | category | flops | bytes accessed | tf_op | source)
XLA Modules:
  0.0 13.1 jit_solution(16474475861136468387)
XLA Ops:
  0.6 11.3 %shard_map.95 = (f32[19,128,128]{2,1,0:T(8,128)S(1)}, f32[2,5,16,128]{3,2,1,0:T(8,128)S(1)}, f32[2,5,8,128]{3,2,1,0:T(8,128)S(1)}, f32[14,8,128]{2,1,0:T(8,128)S(1)}, f32[6,1,128]{2,1,0:T(1,128)S(1)}) custom-call(f32[19,128,128]{2,1,0:T(8,128)} %bitcast.12, f32[128,128]{1,0:T(8,128)} %bitcast.13, s32[128,128]{1,0:T(8,128)} %bitcast.14, s32[1,256]{1,0:T(1,128)} %bitcast.17, ...), custom_call_target="tpu_custom_call" | custom-call | tf_op jit(solution)/shard_map/pallas_call | solution.py:837
  12.0 1.1 %shard_map.96 = (f32[19,128,128]{2,1,0:T(8,128)}, f32[6,1,128]{2,1,0:T(1,128)}) custom-call(f32[19,128,128]{2,1,0:T(8,128)S(1)} %get-tuple-element.9.rel, f32[2,5,16,128]{3,2,1,0:T(8,128)S(1)} %get-tuple-element.10.xhalo, f32[2,5,8,128]{3,2,1,0:T(8,128)S(1)} %get-tuple-element.11.yhalo, f32[14,8,128]{2,1,0:T(8,128)S(1)} %get-tuple-element.12.thalo, ...), custom_call_target="tpu_custom_call" | custom-call | tf_op jit(solution)/shard_map/pallas_call | solution.py:879

commit v4 on v3

--- a/solution.py
+++ b/solution.py
@@ -202,10 +202,8 @@
     def greet(o, vector):
         pl.semaphore_signal(barrier, inc=1, device_id=device(vector), device_id_type=MESH)
 
-    for copy in small_ins:
-        copy.start()
     pops_in(0).start()
-    for copy in cell_ins:
+    for copy in small_ins + cell_ins:
         copy.start()
     for step in range(1, steps):
         pops_in(step).start()

time: 13.3 us -> 13.2 us (level)
  no operation moved by 1% of the time
where the time goes in v4:
time: 13.2 us; the launch traced here: 13.1 us
  Pallas kernels  12.4 us (94%)
  between operations  0.64 us (5%)
    pallas_call x1, Pallas kernels, body(): pl.pallas_call(functools.partial(kernel, sizes, (X, Y, Z)), out_shape=(pl...  11.3 us
    pallas_call x1, Pallas kernels, body(): pl.pallas_call(functools.partial(pass_kernel, sizes, (X, Y, Z)), out_shap...  1.13 us

profile of v4, /device:TPU:0, one launch (start us, length us, event | category | flops | bytes accessed | tf_op | source)
XLA Modules:
  0.0 13.1 jit_solution(15808357018800604163)
XLA Ops:
  0.6 11.3 %shard_map.95 = (f32[19,128,128]{2,1,0:T(8,128)S(1)}, f32[2,5,16,128]{3,2,1,0:T(8,128)S(1)}, f32[2,5,8,128]{3,2,1,0:T(8,128)S(1)}, f32[14,8,128]{2,1,0:T(8,128)S(1)}, f32[6,1,128]{2,1,0:T(1,128)S(1)}) custom-call(f32[19,128,128]{2,1,0:T(8,128)} %bitcast.12, f32[128,128]{1,0:T(8,128)} %bitcast.13, s32[128,128]{1,0:T(8,128)} %bitcast.14, s32[1,256]{1,0:T(1,128)} %bitcast.17, ...), custom_call_target="tpu_custom_call" | custom-call | tf_op jit(solution)/shard_map/pallas_call | solution.py:835
  12.0 1.1 %shard_map.96 = (f32[19,128,128]{2,1,0:T(8,128)}, f32[6,1,128]{2,1,0:T(1,128)}) custom-call(f32[19,128,128]{2,1,0:T(8,128)S(1)} %get-tuple-element.9.rel, f32[2,5,16,128]{3,2,1,0:T(8,128)S(1)} %get-tuple-element.10.xhalo, f32[2,5,8,128]{3,2,1,0:T(8,128)S(1)} %get-tuple-element.11.yhalo, f32[14,8,128]{2,1,0:T(8,128)S(1)} %get-tuple-element.12.thalo, ...), custom_call_target="tpu_custom_call" | custom-call | tf_op jit(solution)/shard_map/pallas_call | solution.py:877
